TPU v7x, 8 devices: a whole 2x2x1 slice. The times are simulated.
8 devices in a mesh: dp: 2 (over z, y), cp: 4 (over x, core).
Axes of the slice: x: 2, y: 2, z: 1, core: 2. Of those that a mesh axis runs over, the one named last changes fastest.
Arguments:
- x: bfloat16 [512, 2048], P(('dp', 'cp')), parts along dimension 0
- k_cache: bfloat16 [32768, 4, 128], P(('dp', 'cp')), parts along dimension 0
- v_cache: bfloat16 [32768, 4, 128], P(('dp', 'cp')), parts along dimension 0
- ln_gain: bfloat16 [2048], replicated
- w_q: bfloat16 [2048, 4096], replicated
- w_k: bfloat16 [2048, 512], replicated
- w_v: bfloat16 [2048, 512], replicated
- w_o: bfloat16 [4096, 2048], replicated
- q_gain: bfloat16 [128], replicated
- k_gain: bfloat16 [128], replicated
Outputs:
- output 1: bfloat16 [512, 2048], P(('dp', 'cp')), parts along dimension 0
- output 2: bfloat16 [512, 4, 128], P(('dp', 'cp')), parts along dimension 0
- output 3: bfloat16 [512, 4, 128], P(('dp', 'cp')), parts along dimension 0
There are 2 independent parts. A program takes and returns all parts, laid end to end along the dimension named above; an argument that names none is the same for every part.
All inputs are finite; a program needn't handle non-finite values.
Results may differ from a plain program's by a relative error of at most 0.0107701.
Values are sent between devices in bfloat16 or wider.
A program may use at most 1 GiB of HBM per device.

v0:
```python
import jax
import jax.numpy as jnp
from jax import lax
from jax.sharding import PartitionSpec as P

HEAD_DIM = 128
ROPE_THETA = 1.0e6
NORM_EPS = 1.0e-6
MASK_VALUE = -1.0e30


def rms_norm(vals, gain):
    mean_sq = jnp.mean(vals * vals, axis=-1, keepdims=True)
    return vals * lax.rsqrt(mean_sq + NORM_EPS) * gain


def apply_rope(vals, positions):
    half = HEAD_DIM // 2
    inv_freq = ROPE_THETA ** (-jnp.arange(half, dtype=jnp.float32) * (2.0 / HEAD_DIM))
    angles = positions.astype(jnp.float32)[:, None] * inv_freq[None, :]
    cos_tab = jnp.cos(angles)[:, None, :]
    sin_tab = jnp.sin(angles)[:, None, :]
    first = vals[..., :half]
    second = vals[..., half:]
    return jnp.concatenate([first * cos_tab - second * sin_tab, second * cos_tab + first * sin_tab], axis=-1)


def project_rows(x_wide, ln_gain, w_q, w_k, w_v, q_gain, k_gain, positions):
    rows = x_wide.shape[0]
    hidden = rms_norm(x_wide, ln_gain.astype(jnp.float32)).astype(jnp.bfloat16)
    q_raw = jnp.dot(hidden, w_q, preferred_element_type=jnp.float32).astype(jnp.bfloat16).reshape(rows, -1, HEAD_DIM)
    k_raw = jnp.dot(hidden, w_k, preferred_element_type=jnp.float32).astype(jnp.bfloat16).reshape(rows, -1, HEAD_DIM)
    v_new = jnp.dot(hidden, w_v, preferred_element_type=jnp.float32).astype(jnp.bfloat16).reshape(rows, -1, HEAD_DIM)
    q_rot = apply_rope(rms_norm(q_raw.astype(jnp.float32), q_gain.astype(jnp.float32)), positions).astype(jnp.bfloat16)
    k_new = apply_rope(rms_norm(k_raw.astype(jnp.float32), k_gain.astype(jnp.float32)), positions).astype(jnp.bfloat16)
    return q_rot, k_new, v_new


def partial_attend(q_grp, keys, vals, allowed):
    scale = HEAD_DIM ** -0.5
    scores = jnp.einsum('rkgd,skd->krgs', q_grp, keys, preferred_element_type=jnp.float32) * scale
    if allowed is not None:
        scores = jnp.where(allowed[None, :, None, :], scores, MASK_VALUE)
    peak = jnp.max(scores, axis=-1)
    weights = jnp.exp(scores - peak[..., None])
    weighted = jnp.einsum('krgs,skd->krgd', weights.astype(jnp.bfloat16), vals, preferred_element_type=jnp.float32)
    return peak, jnp.sum(weights, axis=-1), weighted


def combine_two(first, second):
    peak_a, sum_a, acc_a = first
    peak_b, sum_b, acc_b = second
    top_peak = jnp.maximum(jnp.max(peak_a, axis=0), jnp.max(peak_b, axis=0))
    factor_a = jnp.exp(peak_a - top_peak[None])
    factor_b = jnp.exp(peak_b - top_peak[None])
    total_sum = jnp.sum(factor_a * sum_a, axis=0) + jnp.sum(factor_b * sum_b, axis=0)
    total = jnp.sum(factor_a[..., None] * acc_a, axis=0) + jnp.sum(factor_b[..., None] * acc_b, axis=0)
    return total / total_sum[..., None]


def solution(mesh):
    cp_size = mesh.shape['cp']
    row_spec = P(('dp', 'cp'), None)
    cache_spec = P(('dp', 'cp'), None, None)
    whole = P()

    def device_step(x_rows, k_cache, v_cache, ln_gain, w_q, w_k, w_v, w_o, q_gain, k_gain):
        rows = x_rows.shape[0]
        prefix_len = k_cache.shape[0] * cp_size
        kv_heads = k_cache.shape[1]
        q_heads = w_q.shape[1] // HEAD_DIM
        group = q_heads // kv_heads
        my_index = lax.axis_index('cp')
        row_ids = my_index * rows + jnp.arange(rows)
        key_ids = jnp.arange(rows)
        x_wide = x_rows.astype(jnp.float32)
        q_rot, k_new, v_new = project_rows(x_wide, ln_gain, w_q, w_k, w_v, q_gain, k_gain, prefix_len + row_ids)
        q_grp = q_rot.reshape(rows, kv_heads, group, HEAD_DIM)
        every_q = lax.all_gather(q_grp, 'cp')
        every_k = lax.all_gather(k_new, 'cp')
        every_v = lax.all_gather(v_new, 'cp')

        def block_work(block):
            q_block, k_block, v_block, source = block
            prefix_part = partial_attend(q_block, k_cache, v_cache, None)
            allowed = (source * rows + key_ids)[None, :] <= row_ids[:, None]
            new_part = partial_attend(q_grp, k_block, v_block, allowed)
            return prefix_part, new_part

        prefix_parts, new_parts = lax.map(block_work, (every_q, every_k, every_v, jnp.arange(cp_size)))
        returned = tuple(lax.all_to_all(piece, 'cp', 0, 0, tiled=True) for piece in prefix_parts)
        attended = combine_two(returned, new_parts)
        attended = jnp.transpose(attended, (1, 0, 2, 3)).reshape(rows, q_heads * HEAD_DIM).astype(jnp.bfloat16)
        out = (x_wide + jnp.dot(attended, w_o, preferred_element_type=jnp.float32)).astype(jnp.bfloat16)
        return out, k_new, v_new

    return jax.shard_map(device_step, mesh=mesh, in_specs=(row_spec, cache_spec, cache_spec, whole, whole, whole, whole, whole, whole, whole), out_specs=(row_spec, cache_spec, cache_spec), check_vma=False)
```

profile of v0, /device:TPU:0, one launch (start us, length us, event | category | flops | bytes accessed | tf_op | source)
XLA Modules:
  0.0 338.4 jit_solution(11560747912916597431)
XLA Ops:
  9.2 9.0 %fusion.35 = f32[8,8,32,128]{3,1,2,0:T(8,128)S(1)} fusion(bf16[2048,4096]{1,0:T(8,128)(2,1)} %param.16, bf16[64,2048]{1,0:T(8,128)(2,1)} %param.12, f32[2048]{0:T(1024)S(1)} %convert_element_type.77, f32[64]{0:T(128)S(1)} %add_rsqrt_fusion.2), kind=kOutput, calls=%fused_computation.42 | convolution fusion | flops 1074790400 | bytes 18096384 | tf_op jit(solution)/shard_map/dot_general | solution.py:31
  25.3 4.9 %copy.84 = bf16[4096,4,128]{2,0,1:T(8,128)(2,1)} copy(bf16[4096,4,128]{2,1,0:T(4,128)(2,1)} %param.13) | data formatting | bytes 8388608
  33.1 11.5 %all_gather.11 = bf16[4,64,4,128]{3,1,2,0:T(8,128)(2,1)S(1)} all-gather(bf16[1,64,4,128]{3,1,2,0:T(8,128)(2,1)S(1)} %pad_maximum_fusion.2), channel_id=1, replica_groups=mesh['dp'=2,'cp'=4] {'cp'}, dimensions={0}, use_global_device_ids=true | all-gather | bytes 327680 | tf_op jit(solution)/shard_map/all_gather | solution.py:80
  44.6 8.0 %all_gather.12 = bf16[4,64,4,128]{3,1,2,0:T(8,128)(2,1)S(1)} all-gather(bf16[1,64,4,128]{3,1,2,0:T(8,128)(2,1)S(1)} %copy.80), channel_id=1, replica_groups=mesh['dp'=2,'cp'=4] {'cp'}, dimensions={0}, use_global_device_ids=true | all-gather | bytes 327680 | tf_op jit(solution)/shard_map/all_gather | solution.py:81
  52.9 197.8 %while.21 = (s32[]{:T(128)}, f32[4,4,64,8]{2,3,1,0:T(8,128)}, f32[4,4,64,8]{2,3,1,0:T(8,128)}, f32[4,4,64,8,128]{4,3,2,1,0:T(8,128)}, f32[4,4,64,8]{2,3,1,0:T(8,...) while((s32[]{:T(128)}, f32[4,4,64,8]{2,3,1,0:T(8,128)}, ...), condition=%wide.region_8.9_spmd.clone, body=%wide.region_3.8_spmd.clone.sunk | while | flops 4429967360 | bytes 114909376 | solution.py:90
  57.5 14.8 %multiply_reduce_fusion.8 = (f32[4,64,8]{2,1,0:T(8,128)S(1)}, f32[4,64,8,4096]{3,2,1,0:T(8,128)}) fusion(bf16[4096,4,128]{2,0,1:T(8,128)(2,1)} %get-tuple-element.419, bf16[4,64,4,8,128]{4,3,2,1,0:T(8,128)(2,1)} %get-tuple-element.418, s32[]{:T(128)} %get-tuple-element.394), kind=kOutput, calls=%fused_computation.3.clone.1 | convolution fusion | flops 2164258816 | bytes 38281728 | tf_op jit(solution)/shard_map/while/body/eval_jaxpr/rkgd,skd->krgs/dot_general | solution.py:41
  72.4 14.0 %fusion.70 = f32[4,64,8]{2,1,0:T(8,128)S(1)} fusion(f32[4,64,8,4096]{3,2,1,0:T(8,128)} %get-tuple-element.367, f32[4,64,8]{2,1,0:T(8,128)S(1)} %get-tuple-element.368), kind=kLoop, calls=%fused_computation.5.clone.1 | loop fusion | flops 25163776 | bytes 33570816 | tf_op jit(solution)/shard_map/while/body/eval_jaxpr/reduce_sum | solution.py:47
  87.2 15.2 %fusion.71 = f32[4,4,64,8,128]{4,3,2,1,0:T(8,128)} fusion(f32[4,4,64,8,128]{4,3,2,1,0:T(8,128)} %get-tuple-element.397, s32[]{:T(128)} %get-tuple-element.394, bf16[4096,4,128]{2,0,1:T(8,128)(2,1)} %get-tuple-element.420, f32[4,64,8,4096]{3,2,1,0:T(8,128)} %get-tuple-element.367, f32[4,64,8]{2,1,0:T(8,128)S(1)} %get-tuple-element.368), kind=kOutput, calls=%fused_computation.11.clone.1 | convolution fusion | flops 2172649472 | bytes 38806016 | tf_op jit(solution)/shard_map/while/body/eval_jaxpr/krgs,skd->krgd/dot_general | solution.py:46
  107.0 14.8 %multiply_reduce_fusion.8 = (f32[4,64,8]{2,1,0:T(8,128)S(1)}, f32[4,64,8,4096]{3,2,1,0:T(8,128)}) fusion(bf16[4096,4,128]{2,0,1:T(8,128)(2,1)} %get-tuple-element.419, bf16[4,64,4,8,128]{4,3,2,1,0:T(8,128)(2,1)} %get-tuple-element.418, s32[]{:T(128)} %get-tuple-element.394), kind=kOutput, calls=%fused_computation.3.clone.1 | convolution fusion | flops 2164258816 | bytes 38281728 | tf_op jit(solution)/shard_map/while/body/eval_jaxpr/rkgd,skd->krgs/dot_general | solution.py:41
  121.8 14.0 %fusion.70 = f32[4,64,8]{2,1,0:T(8,128)S(1)} fusion(f32[4,64,8,4096]{3,2,1,0:T(8,128)} %get-tuple-element.367, f32[4,64,8]{2,1,0:T(8,128)S(1)} %get-tuple-element.368), kind=kLoop, calls=%fused_computation.5.clone.1 | loop fusion | flops 25163776 | bytes 33570816 | tf_op jit(solution)/shard_map/while/body/eval_jaxpr/reduce_sum | solution.py:47
  136.7 15.2 %fusion.71 = f32[4,4,64,8,128]{4,3,2,1,0:T(8,128)} fusion(f32[4,4,64,8,128]{4,3,2,1,0:T(8,128)} %get-tuple-element.397, s32[]{:T(128)} %get-tuple-element.394, bf16[4096,4,128]{2,0,1:T(8,128)(2,1)} %get-tuple-element.420, f32[4,64,8,4096]{3,2,1,0:T(8,128)} %get-tuple-element.367, f32[4,64,8]{2,1,0:T(8,128)S(1)} %get-tuple-element.368), kind=kOutput, calls=%fused_computation.11.clone.1 | convolution fusion | flops 2172649472 | bytes 38806016 | tf_op jit(solution)/shard_map/while/body/eval_jaxpr/krgs,skd->krgd/dot_general | solution.py:46
  156.5 14.8 %multiply_reduce_fusion.8 = (f32[4,64,8]{2,1,0:T(8,128)S(1)}, f32[4,64,8,4096]{3,2,1,0:T(8,128)}) fusion(bf16[4096,4,128]{2,0,1:T(8,128)(2,1)} %get-tuple-element.419, bf16[4,64,4,8,128]{4,3,2,1,0:T(8,128)(2,1)} %get-tuple-element.418, s32[]{:T(128)} %get-tuple-element.394), kind=kOutput, calls=%fused_computation.3.clone.1 | convolution fusion | flops 2164258816 | bytes 38281728 | tf_op jit(solution)/shard_map/while/body/eval_jaxpr/rkgd,skd->krgs/dot_general | solution.py:41
  171.3 14.0 %fusion.70 = f32[4,64,8]{2,1,0:T(8,128)S(1)} fusion(f32[4,64,8,4096]{3,2,1,0:T(8,128)} %get-tuple-element.367, f32[4,64,8]{2,1,0:T(8,128)S(1)} %get-tuple-element.368), kind=kLoop, calls=%fused_computation.5.clone.1 | loop fusion | flops 25163776 | bytes 33570816 | tf_op jit(solution)/shard_map/while/body/eval_jaxpr/reduce_sum | solution.py:47
  186.1 15.2 %fusion.71 = f32[4,4,64,8,128]{4,3,2,1,0:T(8,128)} fusion(f32[4,4,64,8,128]{4,3,2,1,0:T(8,128)} %get-tuple-element.397, s32[]{:T(128)} %get-tuple-element.394, bf16[4096,4,128]{2,0,1:T(8,128)(2,1)} %get-tuple-element.420, f32[4,64,8,4096]{3,2,1,0:T(8,128)} %get-tuple-element.367, f32[4,64,8]{2,1,0:T(8,128)S(1)} %get-tuple-element.368), kind=kOutput, calls=%fused_computation.11.clone.1 | convolution fusion | flops 2172649472 | bytes 38806016 | tf_op jit(solution)/shard_map/while/body/eval_jaxpr/krgs,skd->krgd/dot_general | solution.py:46
  205.9 14.8 %multiply_reduce_fusion.8 = (f32[4,64,8]{2,1,0:T(8,128)S(1)}, f32[4,64,8,4096]{3,2,1,0:T(8,128)}) fusion(bf16[4096,4,128]{2,0,1:T(8,128)(2,1)} %get-tuple-element.419, bf16[4,64,4,8,128]{4,3,2,1,0:T(8,128)(2,1)} %get-tuple-element.418, s32[]{:T(128)} %get-tuple-element.394), kind=kOutput, calls=%fused_computation.3.clone.1 | convolution fusion | flops 2164258816 | bytes 38281728 | tf_op jit(solution)/shard_map/while/body/eval_jaxpr/rkgd,skd->krgs/dot_general | solution.py:41
  220.8 14.0 %fusion.70 = f32[4,64,8]{2,1,0:T(8,128)S(1)} fusion(f32[4,64,8,4096]{3,2,1,0:T(8,128)} %get-tuple-element.367, f32[4,64,8]{2,1,0:T(8,128)S(1)} %get-tuple-element.368), kind=kLoop, calls=%fused_computation.5.clone.1 | loop fusion | flops 25163776 | bytes 33570816 | tf_op jit(solution)/shard_map/while/body/eval_jaxpr/reduce_sum | solution.py:47
  235.6 15.2 %fusion.71 = f32[4,4,64,8,128]{4,3,2,1,0:T(8,128)} fusion(f32[4,4,64,8,128]{4,3,2,1,0:T(8,128)} %get-tuple-element.397, s32[]{:T(128)} %get-tuple-element.394, bf16[4096,4,128]{2,0,1:T(8,128)(2,1)} %get-tuple-element.420, f32[4,64,8,4096]{3,2,1,0:T(8,128)} %get-tuple-element.367, f32[4,64,8]{2,1,0:T(8,128)S(1)} %get-tuple-element.368), kind=kOutput, calls=%fused_computation.11.clone.1 | convolution fusion | flops 2172649472 | bytes 38806016 | tf_op jit(solution)/shard_map/while/body/eval_jaxpr/krgs,skd->krgd/dot_general | solution.py:46
  252.3 3.3 all-to-all-start
  259.3 6.3 %all_to_all.15 = f32[4,1,2048]{2,1,0:T(1,128)S(1)} all-to-all(f32[4,1,2048]{2,1,0:T(1,128)S(1)} %reshape.224), channel_id=1, replica_groups=mesh['dp'=2,'cp'=4] {'cp'}, dimensions={0} | all-to-all | bytes 65536 | tf_op jit(solution)/shard_map/all_to_all | solution.py:91
  265.6 5.2 %all-to-all-start.1 = ((f32[4,4,64,8,128]{4,3,2,1,0:T(8,128)}), f32[4,4,64,8,128]{4,3,2,1,0:T(8,128)}, u32[]{:S(2)}, u32[]{:S(2)}) async-start(f32[4,4,64,8,128]{4,3,2,1,0:T(8,128)} %get-tuple-element.92), calls=%async_computation.1 | async-start | bytes 8388608 | tf_op jit(solution)/shard_map/all_to_all | solution.py:91
  275.0 2.9 multiply_reduce_fusion.1
  278.0 40.5 %all-to-all-done.1 = f32[4,4,64,8,128]{4,3,2,1,0:T(8,128)} async-done(((f32[4,4,64,8,128]{4,3,2,1,0:T(8,128)}), f32[4,4,64,8,128]{4,3,2,1,0:T(8,128)}, u32[]{:S(2)}, u32[]{:S(2)}) %all-to-all-start.1) | async-done | bytes 4194336 | tf_op jit(solution)/shard_map/all_to_all | solution.py:91
  318.5 2.9 multiply_reduce_fusion.2
  321.9 9.6 %fusion.34 = bf16[64,2048]{1,0:T(8,128)(2,1)} fusion(bf16[4096,2048]{1,0:T(8,128)(2,1)} %param.19, bf16[64,2048]{1,0:T(8,128)(2,1)S(1)} %copy-done.3, bf16[8,8,32,128]{3,2,1,0:T(8,128)(2,1)S(1)} %bitcast.128), kind=kOutput, calls=%fused_computation.41 | convolution fusion | flops 1074135040 | bytes 17825792 | tf_op jit(solution)/shard_map/dot_general | solution.py:94
  (138 shorter events, 40.5 us)
Async XLA Ops:
  7.2 15.2 %copy-start = (bf16[2048,512]{1,0:T(8,128)(2,1)S(1)}, bf16[2048,512]{1,0:T(8,128)(2,1)}, u32[]{:S(2)}) copy-start(bf16[2048,512]{1,0:T(8,128)(2,1)} %param.17) | copy-start | bytes 6291460
  7.2 45.7 %all-gather.2.cloned.1.call-start = ((), (), s32[]{:S(2)}) async-start(), calls=%async_computation.3 | async-start | bytes 2621440 | tf_op jit(solution)/shard_map/all_gather | solution.py:79
  9.2 9.6 %copy-start.13 = (bf16[128]{0:T(256)(128)(2,1)S(1)}, bf16[128]{0:T(256)(128)(2,1)}, u32[]{:S(2)}) copy-start(bf16[128]{0:T(256)(128)(2,1)} %param.20) | copy-start | bytes 772
  19.2 3.2 copy-start.2
  19.9 3.2 copy-start.14
  25.3 5.0 %copy-start.10 = (bf16[64,512]{1,0:T(8,128)(2,1)}, bf16[64,512]{1,0:T(8,128)(2,1)S(1)}, u32[]{:S(2)}) copy-start(bf16[64,512]{1,0:T(8,128)(2,1)S(1)} %convolution_convert_fusion.1) | copy-start | bytes 196612
  25.3 4.9 %copy-start.4 = (bf16[4096,4,128]{2,1,0:T(4,128)(2,1)S(1)}, bf16[4096,4,128]{2,1,0:T(4,128)(2,1)}, u32[]{:S(2)}) copy-start(bf16[4096,4,128]{2,1,0:T(4,128)(2,1)} %param.14) | copy-start | bytes 12582916
  30.3 22.3 %copy-start.5 = (bf16[64,4,8,64]{3,0,2,1:T(8,128)(2,1)S(1)}, bf16[64,4,8,64]{3,0,2,1:T(8,128)(2,1)}, u32[]{:S(2)}) copy-start(bf16[64,4,8,64]{3,0,2,1:T(8,128)(2,1)} %copy.78) | copy-start | bytes 786436
  33.0 19.9 %copy-start.6 = (bf16[64,4,64]{2,0,1:T(8,128)(2,1)}, bf16[64,4,64]{2,0,1:T(8,128)(2,1)S(1)}, u32[]{:S(2)}) copy-start(bf16[64,4,64]{2,0,1:T(8,128)(2,1)S(1)} %get-tuple-element.260) | copy-start | bytes 98308
  33.0 19.9 %copy-start.8 = (bf16[64,4,64]{2,0,1:T(8,128)(2,1)}, bf16[64,4,64]{2,0,1:T(8,128)(2,1)S(1)}, u32[]{:S(2)}) copy-start(bf16[64,4,64]{2,0,1:T(8,128)(2,1)S(1)} %get-tuple-element.261) | copy-start | bytes 98308
  252.3 7.0 %all-to-all-start = ((f32[4,1,2048]{2,1,0:T(1,128)}), f32[4,1,2048]{2,1,0:T(1,128)S(1)}, u32[]{:S(2)}, u32[]{:S(2)}) async-start(f32[4,1,2048]{2,1,0:T(1,128)} %reshape.222), calls=%async_computation | async-start | bytes 65536 | tf_op jit(solution)/shard_map/all_to_all | solution.py:91
  265.6 5.2 %copy-start.11 = (bf16[64,512]{1,0:T(8,128)(2,1)S(1)}, bf16[64,512]{1,0:T(8,128)(2,1)}, u32[]{:S(2)}) copy-start(bf16[64,512]{1,0:T(8,128)(2,1)} %copy-done.10) | copy-start | bytes 196612
  265.6 5.9 %copy-start.7 = (bf16[64,4,64]{2,0,1:T(8,128)(2,1)S(1)}, bf16[64,4,64]{2,0,1:T(8,128)(2,1)}, u32[]{:S(2)}) copy-start(bf16[64,4,64]{2,0,1:T(8,128)(2,1)} %copy-done.6) | copy-start | bytes 98308
  265.6 5.9 %copy-start.9 = (bf16[64,4,64]{2,0,1:T(8,128)(2,1)S(1)}, bf16[64,4,64]{2,0,1:T(8,128)(2,1)}, u32[]{:S(2)}) copy-start(bf16[64,4,64]{2,0,1:T(8,128)(2,1)} %copy-done.8) | copy-start | bytes 98308
  265.6 8.8 %copy-start.12 = (f32[4,4,64,8]{2,3,1,0:T(8,128)S(1)}, f32[4,4,64,8]{2,3,1,0:T(8,128)}, u32[]{:S(2)}) copy-start(f32[4,4,64,8]{2,3,1,0:T(8,128)} %get-tuple-element.95) | copy-start | bytes 98308
  265.6 52.9 %all-to-all-start.1 = ((f32[4,4,64,8,128]{4,3,2,1,0:T(8,128)}), f32[4,4,64,8,128]{4,3,2,1,0:T(8,128)}, u32[]{:S(2)}, u32[]{:S(2)}) async-start(f32[4,4,64,8,128]{4,3,2,1,0:T(8,128)} %get-tuple-element.92), calls=%async_computation.1 | async-start | bytes 8388608 | tf_op jit(solution)/shard_map/all_to_all | solution.py:91
  277.9 43.9 %copy-start.3 = (bf16[64,2048]{1,0:T(8,128)(2,1)S(1)}, bf16[64,2048]{1,0:T(8,128)(2,1)}, u32[]{:S(2)}) copy-start(bf16[64,2048]{1,0:T(8,128)(2,1)} %param.12) | copy-start | bytes 786436
  321.9 9.7 %copy-start.1 = (bf16[2048,512]{1,0:T(8,128)(2,1)S(1)}, bf16[2048,512]{1,0:T(8,128)(2,1)}, u32[]{:S(2)}) copy-start(bf16[2048,512]{1,0:T(8,128)(2,1)} %param.17) | copy-start | bytes 6291460
Sparse Core Ops, SparseCore 0:
  21.2 23.5 all-gather.1
where the time goes:
time: 339 us; the launch traced here: 338 us
  matrix products  149 us (44%)
  other arithmetic  70.4 us (21%)
  waiting for transfers between devices  43.3 us (13%)
  blocking collectives  25.8 us (8%)
  local copies, waits for them, and re-layouts  23.7 us (7%)
  between operations  14.5 us (4%)
  starting transfers between devices  8.52 us (3%)
    dot_general x8, matrix products, partial_attend(): jnp.einsum('krgs,skd->krgd', weights.astype(jnp.bfloat16), vals, preferre...  66 us
    dot_general x8, matrix products, partial_attend(): jnp.einsum('rkgd,skd->krgs', q_grp, keys, preferred_element_type=jnp.floa...  61.9 us
    reduce_sum x4, other arithmetic, partial_attend(): return (peak, jnp.sum(weights, axis=-1), weighted)  56.1 us
    all_to_all x2, waiting for transfers between devices, device_step(): lax.all_to_all(piece, 'cp', 0, 0, tiled=True)  43.3 us
    all_gather x1, blocking collectives, device_step(): every_k = lax.all_gather(k_new, 'cp')  11.5 us
    unnamed x38, local copies, waits for them, and re-layouts  11 us
    dot_general x1, matrix products, device_step(): jnp.dot(attended, w_o, preferred_element_type=jnp.float32)  9.64 us
    dot_general x1, matrix products, project_rows(): jnp.dot(hidden, w_q, preferred_element_type=jnp.float32)  9 us
  transfers between devices with their start and end apart: 3, of which 2 were waited for; matrix products, arithmetic and copies ran while one was open for 6% of the time, Pallas kernels for 0%

commit v1 on v0

v1 whole, which is shorter than its diff:
```python
import functools

import jax
import jax.numpy as jnp
import numpy as np
from jax import lax
from jax.experimental import pallas as pl
from jax.experimental.pallas import tpu as pltpu
from jax.sharding import PartitionSpec as P

HEAD_DIM = 128
HALF = HEAD_DIM // 2
ROPE_THETA = 1.0e6
NORM_EPS = 1.0e-6
LOG2E = 1.4426950408889634
SCALE2 = HEAD_DIM ** -0.5 * LOG2E
MESH = pl.DeviceIdType.MESH
F32 = jnp.float32
BF16 = jnp.bfloat16
ROWS = 64
CP = 4
KEYS = 4096
ALL_KEYS = KEYS + ROWS
KV = 4
GROUPS = 8
COLS = 256
TILE = 256
MSG = HEAD_DIM + 8
HIDDEN = 2048
CHUNK = 256


def rope_tables(prefix_len):
    freq = (ROPE_THETA ** (-np.arange(HALF, dtype=np.float64) * (2.0 / HEAD_DIM))).astype(np.float32)
    pos = (prefix_len + np.arange(CP * ROWS)).astype(np.float32).reshape(CP, 1, ROWS)
    angles = (pos * freq[None, :, None]).astype(np.float32)
    angles = np.concatenate([angles, angles], axis=2).astype(np.float64)
    return np.cos(angles).astype(np.float32), np.sin(angles).astype(np.float32)


def kernel(x_hbm, k_hbm, v_hbm, ln_ref, wq_hbm, wk_hbm, wv_hbm, wo_hbm, qg_ref, kg_ref, cos_ref, sin_ref,
           out_ref, knew_ref, vnew_ref,
           xall, hbuf, wbuf, wk, wv, kst, vst, kf, vf, ks, vt, qt, gq, gk, s_a, s_b, m_a, m_b,
           abuf, bbuf, rbuf, cbuf, obuf,
           x_sem, xs_sem, xr_sem, w_sem, kv_sem, cache_sem, wo_sem, as_sem, ar_sem, cs_sem, cr_sem):
    me = lax.axis_index("cp")
    dp = lax.axis_index("dp")
    partner = me + 1 - 2 * lax.rem(me, 2)
    cross = lax.rem(me + 2, CP)
    far = lax.rem(partner + 2, CP)

    def remote(src, dst, ssem, rsem, to):
        return pltpu.make_async_remote_copy(src_ref=src, dst_ref=dst, send_sem=ssem, recv_sem=rsem,
                                            device_id=(dp, to), device_id_type=MESH)

    x_copy = pltpu.make_async_copy(x_hbm, xall.at[0], x_sem)
    x_copy.start()
    wk_copy = pltpu.make_async_copy(wk_hbm, wk, kv_sem.at[0])
    wv_copy = pltpu.make_async_copy(wv_hbm, wv, kv_sem.at[1])

    def wq_copy(g):
        return pltpu.make_async_copy(wq_hbm.at[:, pl.ds(pl.multiple_of(g * 512, 512), 512)], wbuf.at[g], w_sem.at[g])

    def wo_copy(b):
        nb = b // 2
        kh = b % 2
        return pltpu.make_async_copy(wo_hbm.at[pl.ds(kh * 2048, 2048), pl.ds(nb * 512, 512)], wbuf.at[b], wo_sem.at[b])

    NC = 4
    CB = KEYS // NC

    def cache_copy(src, dst, j, n):
        return pltpu.make_async_copy(src.at[pl.ds(j * CB, CB)], dst.at[pl.ds(j * CB, CB)], cache_sem.at[n, j])

    for g in range(4):
        wq_copy(g).start()
    wk_copy.start()
    wv_copy.start()
    for g in range(4, GROUPS):
        wq_copy(g).start()
    for j in range(NC):
        cache_copy(k_hbm, kst, j, 0).start()
        cache_copy(v_hbm, vst, j, 1).start()

    barrier = pltpu.get_barrier_semaphore()
    for to in (partner, cross):
        pl.semaphore_signal(barrier, inc=1, device_id=(dp, to), device_id_type=MESH)
    pl.semaphore_wait(barrier, 2)
    x_copy.wait()
    x_to_cross = remote(xall.at[0], xall.at[2], xs_sem.at[1], xr_sem.at[1], cross)
    x_to_cross.start()
    x_to_partner = remote(xall.at[0], xall.at[1], xs_sem.at[0], xr_sem.at[0], partner)
    x_to_partner.start()
    x_forward = remote(xall.at[2], xall.at[3], xs_sem.at[2], xr_sem.at[2], partner)

    gq[...] = jnp.broadcast_to(qg_ref[...].astype(F32), (HEAD_DIM, HEAD_DIM)).T
    gk[...] = jnp.broadcast_to(kg_ref[...].astype(F32), (HEAD_DIM, HEAD_DIM)).T
    ln_gain = ln_ref[...].astype(F32)

    def normalise(slot):
        wide = xall[slot].astype(F32)
        mean_sq = jnp.mean(wide * wide, axis=-1, keepdims=True)
        hbuf[slot * ROWS:(slot + 1) * ROWS, :] = (wide * lax.rsqrt(mean_sq + NORM_EPS) * ln_gain).astype(BF16)

    def norm_rope(raw_t, gain, cos, sin):
        z = raw_t.astype(F32)
        mean_sq = jnp.mean(z * z, axis=0, keepdims=True)
        y = z * lax.rsqrt(mean_sq + NORM_EPS) * gain
        first, second = y[:HALF], y[HALF:]
        return jnp.concatenate([first * cos - second * sin, second * cos + first * sin], axis=0).astype(BF16)

    def project(pair, g):
        if isinstance(pair, int) and pair == 0:
            ids, units = (me, partner), (16 + 2 * g + 1, 16 + 2 * g)
        else:
            ids, units = (cross, far), (2 * g + 1, 2 * g)
        raw = jnp.dot(hbuf[pair * 128:(pair + 1) * 128, :], wbuf[g], preferred_element_type=F32).astype(BF16)
        for n in range(2):
            cos, sin = cos_ref[ids[n]], sin_ref[ids[n]]
            part = raw[n * ROWS:(n + 1) * ROWS]
            for hh in range(2):
                two = jnp.concatenate([part[:, hh * 256:hh * 256 + 128], part[:, hh * 256 + 128:hh * 256 + 256]], axis=0)
                qt[units[n], :, hh * 128:(hh + 1) * 128] = norm_rope(two.T, gq[...], cos, sin)

    normalise(0)
    x_to_partner.wait_recv()
    normalise(1)

    def pair0(g, carry):
        wq_copy(g).wait()
        project(0, g)
        return carry

    lax.fori_loop(0, GROUPS, pair0, 0)

    wk_copy.wait()
    wv_copy.wait()
    k_raw = jnp.dot(hbuf[0:ROWS, :], wk[...], preferred_element_type=F32).astype(BF16)
    v_raw = jnp.dot(hbuf[0:ROWS, :], wv[...], preferred_element_type=F32).astype(BF16)
    for hh in range(2):
        two = jnp.concatenate([k_raw[:, hh * 256:hh * 256 + 128], k_raw[:, hh * 256 + 128:hh * 256 + 256]], axis=0)
        back = norm_rope(two.T, gk[...], cos_ref[me], sin_ref[me]).T
        for n in range(2):
            ks[2 * hh + n, KEYS:ALL_KEYS, :] = back[n * ROWS:(n + 1) * ROWS]
            knew_ref[:, 2 * hh + n, :] = back[n * ROWS:(n + 1) * ROWS]
    for h in range(KV):
        one = v_raw[:, h * 128:(h + 1) * 128]
        vt[h, :, KEYS:ALL_KEYS] = one.T
        vnew_ref[:, h, :] = one

    x_to_cross.wait_recv()
    x_forward.start()
    for j in range(NC):
        cache_copy(k_hbm, kst, j, 0).wait()
        cache_copy(v_hbm, vst, j, 1).wait()

        def relayout(i, carry, j=j):
            at = pl.ds(pl.multiple_of(j * CB + i * CHUNK, CHUNK), CHUNK)
            kf[...] = kst[at].astype(F32).reshape(CHUNK * KV, HEAD_DIM)
            vf[...] = vst[at].astype(F32).reshape(CHUNK * KV, HEAD_DIM)
            for h in range(KV):
                ks[h, at, :] = kf[pl.ds(h, CHUNK, stride=KV), :].astype(BF16)
                vt[h, :, at] = vf[pl.ds(h, CHUNK, stride=KV), :].astype(BF16).T
            return carry

        lax.fori_loop(0, CB // CHUNK, relayout, 0)

    normalise(2)
    x_forward.wait_recv()
    normalise(3)

    def pair1(g, carry):
        project(1, g)
        return carry

    lax.fori_loop(0, GROUPS, pair1, 0)
    for b in range(GROUPS):
        wo_copy(b).start()

    tiles = [(t * TILE, TILE) for t in range(KEYS // TILE)] + [(KEYS, ROWS)]

    def colmax(s, n):
        return jnp.max(s.reshape(n // 8, 8, COLS), axis=0)

    class Unit:
        pass

    def begin(u, s_ref, m_ref, dest):
        z = Unit()
        z.s, z.m = s_ref, m_ref
        z.peak = m_ref[0:1]
        z.head = lax.rem(u // 2, GROUPS) // 2
        z.acc = z.sum = None
        return z

    def begin_next(z, u, s_ref, m_ref, dest):
        z.s, z.m = s_ref, m_ref
        z.next_head = lax.rem(u // 2, GROUPS) // 2
        z.q = qt[u]
        z.dest = dest
        z.top = None
        return z

    def weigh(z, t):
        lo, n = tiles[t]
        p = jnp.exp2(z.s[lo:lo + n, :] * SCALE2 - z.peak)
        part = jnp.sum(p.reshape(n // 8, 8, COLS), axis=0)
        z.sum = part if z.sum is None else z.sum + part
        a = jnp.dot(vt[z.head, :, lo:lo + n], p.astype(BF16), preferred_element_type=F32)
        z.acc = a if z.acc is None else z.acc + a

    def score(z, t):
        lo, n = tiles[t]
        s = jnp.dot(ks[z.next_head, lo:lo + n, :], z.q, preferred_element_type=F32)
        if t == len(tiles) - 1:
            key = me * ROWS + lax.broadcasted_iota(jnp.int32, (n, COLS), 0)
            row = z.dest * ROWS + (lax.broadcasted_iota(jnp.int32, (n, COLS), 1) & (ROWS - 1))
            s = jnp.where(key <= row, s, -jnp.inf)
        z.s[lo:lo + n, :] = s
        top = colmax(s, n)
        z.top = top if z.top is None else jnp.maximum(z.top, top)

    def end_next(z):
        z.m[0:1] = jnp.max(z.top, axis=0, keepdims=True) * SCALE2

    def finish(z, ref, slot):
        ref[slot, 0:HEAD_DIM, :] = z.acc
        ref[slot, HEAD_DIM:HEAD_DIM + 1, :] = z.peak
        ref[slot, HEAD_DIM + 1:HEAD_DIM + 2, :] = jnp.sum(z.sum, axis=0, keepdims=True)

    def dests(i):
        return jnp.where(i < GROUPS, far, partner), jnp.where(i < GROUPS, cross, me)

    za, zb = Unit(), Unit()
    da, db = far, cross
    begin_next(za, 0, s_a, m_a, da)
    begin_next(zb, 1, s_b, m_b, db)
    for t in range(len(tiles)):
        score(za, t)
        score(zb, t)
    end_next(za)
    end_next(zb)

    def to_partner(i):
        return remote(abuf.at[i], rbuf.at[i], as_sem.at[i], ar_sem.at[i], partner)

    def to_cross(g):
        return remote(bbuf.at[g], cbuf.at[g], cs_sem.at[g], cr_sem.at[g], cross)

    def combine_cross(g):
        to_partner(g).wait_recv()
        m1, m2 = bbuf[g, 128:129, :], rbuf[g, 128:129, :]
        m = jnp.maximum(m1, m2)
        w1, w2 = jnp.exp2(m1 - m), jnp.exp2(m2 - m)
        bbuf[g, 0:128, :] = bbuf[g, 0:128, :] * w1 + rbuf[g, 0:128, :] * w2
        total = bbuf[g, 129:130, :] * w1 + rbuf[g, 129:130, :] * w2
        bbuf[g, 128:129, :] = m
        bbuf[g, 129:130, :] = total
        to_cross(g).start()

    def attend(i, last):
        a = begin(2 * i, s_a, m_a, None)
        b = begin(2 * i + 1, s_b, m_b, None)
        if not last:
            da, db = dests(i + 1)
            begin_next(a, 2 * i + 2, s_a, m_a, da)
            begin_next(b, 2 * i + 3, s_b, m_b, db)
        for t in range(len(tiles)):
            for z in (a, b):
                weigh(z, t)
                if not last:
                    score(z, t)
        finish(a, abuf, i)
        finish(b, bbuf, i)
        if not last:
            end_next(a)
            end_next(b)
        to_partner(i).start()

    def body(i, carry):
        @pl.when(jnp.logical_and(i >= 2, i < GROUPS + 2))
        def _():
            combine_cross(i - 2)

        attend(i, False)
        return carry

    lax.fori_loop(0, 2 * GROUPS - 1, body, 0)
    attend(2 * GROUPS - 1, True)

    for g in range(GROUPS):
        to_partner(GROUPS + g).wait_recv()
        to_cross(g).wait_recv()
        parts = ((bbuf, GROUPS + g), (rbuf, GROUPS + g), (cbuf, g))
        peaks = [ref[n, 128:129, :] for ref, n in parts]
        m = jnp.maximum(jnp.maximum(peaks[0], peaks[1]), peaks[2])
        ws = [jnp.exp2(p - m) for p in peaks]
        total = sum(ref[n, 129:130, :] * w for (ref, n), w in zip(parts, ws))
        inv = 1.0 / total
        o = sum(ref[n, 0:128, :] * (w * inv) for (ref, n), w in zip(parts, ws)).astype(BF16)
        for hh in range(2):
            rows = o[:, hh * 128:(hh + 1) * 128].T
            for n in range(2):
                col = (4 * g + 2 * hh + n) * HEAD_DIM
                obuf[:, col:col + HEAD_DIM] = rows[n * ROWS:(n + 1) * ROWS]

    for b in range(GROUPS):
        wo_copy(b).wait()
    for nb in range(4):
        cols = slice(nb * 512, (nb + 1) * 512)
        acc = jnp.dot(obuf[:, 0:2048], wbuf[2 * nb], preferred_element_type=F32)
        acc = acc + jnp.dot(obuf[:, 2048:4096], wbuf[2 * nb + 1], preferred_element_type=F32)
        out_ref[:, cols] = (xall[0, :, cols].astype(F32) + acc).astype(BF16)

    x_to_partner.wait_send()
    x_to_cross.wait_send()
    x_forward.wait_send()

    def drain(i, carry):
        to_partner(i).wait_send()
        return carry

    lax.fori_loop(0, 2 * GROUPS, drain, 0)

    def drain_cross(g, carry):
        to_cross(g).wait_send()
        return carry

    lax.fori_loop(0, GROUPS, drain_cross, 0)


def solution(mesh):
    row_spec = P(('dp', 'cp'), None)
    cache_spec = P(('dp', 'cp'), None, None)
    whole = P()
    any_spec = pl.BlockSpec(memory_space=pl.ANY)
    vmem_spec = pl.BlockSpec(memory_space=pltpu.VMEM)

    def device_step(x_rows, k_cache, v_cache, ln_gain, w_q, w_k, w_v, w_o, q_gain, k_gain):
        cos, sin = rope_tables(k_cache.shape[0] * CP)
        dma = pltpu.SemaphoreType.DMA
        return pl.pallas_call(
            kernel,
            out_shape=(jax.ShapeDtypeStruct((ROWS, HIDDEN), BF16),
                       jax.ShapeDtypeStruct((ROWS, KV, HEAD_DIM), BF16),
                       jax.ShapeDtypeStruct((ROWS, KV, HEAD_DIM), BF16)),
            in_specs=[any_spec, any_spec, any_spec, vmem_spec, any_spec, any_spec, any_spec, any_spec,
                      vmem_spec, vmem_spec, vmem_spec, vmem_spec],
            out_specs=(vmem_spec, vmem_spec, vmem_spec),
            scratch_shapes=[
                pltpu.VMEM((4, ROWS, HIDDEN), BF16),
                pltpu.VMEM((4 * ROWS, HIDDEN), BF16),
                pltpu.VMEM((GROUPS, 2048, 512), BF16),
                pltpu.VMEM((HIDDEN, 512), BF16),
                pltpu.VMEM((HIDDEN, 512), BF16),
                pltpu.VMEM((KEYS, KV, HEAD_DIM), BF16),
                pltpu.VMEM((KEYS, KV, HEAD_DIM), BF16),
                pltpu.VMEM((CHUNK * KV, HEAD_DIM), F32),
                pltpu.VMEM((CHUNK * KV, HEAD_DIM), F32),
                pltpu.VMEM((KV, ALL_KEYS, HEAD_DIM), BF16),
                pltpu.VMEM((KV, HEAD_DIM, ALL_KEYS), BF16),
                pltpu.VMEM((4 * GROUPS, HEAD_DIM, COLS), BF16),
                pltpu.VMEM((HEAD_DIM, HEAD_DIM), F32),
                pltpu.VMEM((HEAD_DIM, HEAD_DIM), F32),
                pltpu.VMEM((ALL_KEYS, COLS), F32),
                pltpu.VMEM((ALL_KEYS, COLS), F32),
                pltpu.VMEM((8, COLS), F32),
                pltpu.VMEM((8, COLS), F32),
                pltpu.VMEM((2 * GROUPS, MSG, COLS), F32),
                pltpu.VMEM((2 * GROUPS, MSG, COLS), F32),
                pltpu.VMEM((2 * GROUPS, MSG, COLS), F32),
                pltpu.VMEM((GROUPS, MSG, COLS), F32),
                pltpu.VMEM((ROWS, 4096), BF16),
                dma, dma((3,)), dma((3,)), dma((GROUPS,)), dma((2,)), dma((2, 4)), dma((GROUPS,)),
                dma((2 * GROUPS,)), dma((2 * GROUPS,)), dma((GROUPS,)), dma((GROUPS,)),
            ],
            compiler_params=pltpu.CompilerParams(collective_id=0, has_side_effects=True,
                                                 vmem_limit_bytes=67043328),
        )(x_rows, k_cache, v_cache, ln_gain.reshape(1, -1), w_q, w_k, w_v, w_o,
          q_gain.reshape(1, -1), k_gain.reshape(1, -1), jnp.asarray(cos), jnp.asarray(sin))

    return jax.shard_map(device_step, mesh=mesh,
                         in_specs=(row_spec, cache_spec, cache_spec, whole, whole, whole, whole, whole, whole, whole),
                         out_specs=(row_spec, cache_spec, cache_spec), check_vma=False)
```

time: 339 us -> 72.3 us (0.21)
  matrix products: 149 us -> 0 us
  other arithmetic: 70.4 us -> 0 us
  Pallas kernels: 0 us -> 65.5 us
  waiting for transfers between devices: 43.3 us -> 0 us
  blocking collectives: 25.8 us -> 0 us
  local copies, waits for them, and re-layouts: 23.7 us -> 5.94 us
  between operations: 14.5 us -> 0.64 us
  starting transfers between devices: 8.52 us -> 0 us
    dot_general x20 -> x0, matrix products: 149 us -> none  [the longest x8 66 us: partial_attend(): jnp.einsum('krgs,skd->krgd', weights.astype(jnp.bfloat16), vals, preferre...]
    pallas_call x0 -> x1, Pallas kernels: none -> 65.5 us  [device_step(): pl.pallas_call(kernel, out_shape=(jax.ShapeDtypeStruct((ROWS, HIDDEN), BF...]
    reduce_sum x10 -> x0, other arithmetic: 63.6 us -> none  [the longest x4 56.1 us: partial_attend(): return (peak, jnp.sum(weights, axis=-1), weighted)]
    all_to_all x2 -> x0, waiting for transfers between devices: 43.3 us -> none  [device_step(): lax.all_to_all(piece, 'cp', 0, 0, tiled=True)]
    all_gather x2 -> x0, blocking collectives: 19.5 us -> none  [the longest x1 11.5 us: device_step(): every_k = lax.all_gather(k_new, 'cp')]
    all_to_all x2 -> x0, starting transfers between devices: 8.48 us -> none  [device_step(): lax.all_to_all(piece, 'cp', 0, 0, tiled=True)]
    unnamed x38 -> x3, local copies, waits for them, and re-layouts: 11 us -> 4.65 us
    all_to_all x1 -> x0, blocking collectives: 6.29 us -> none  [device_step(): lax.all_to_all(piece, 'cp', 0, 0, tiled=True)]
  transfers between devices with their start and end apart: 3 -> 0, of which waited for: 2 -> 0; matrix products, arithmetic and copies ran while one was open for 6% -> 0% of each run, Pallas kernels for 0% -> 0%
where the time goes in v1:
time: 72.3 us; the launch traced here: 72.1 us
  Pallas kernels  65.5 us (91%)
  local copies, waits for them, and re-layouts  5.94 us (8%)
    pallas_call x1, Pallas kernels, device_step(): pl.pallas_call(kernel, out_shape=(jax.ShapeDtypeStruct((ROWS, HIDDEN), BF...  65.5 us
    unnamed x3, local copies, waits for them, and re-layouts  4.65 us

profile of v1, /device:TPU:0, one launch (start us, length us, event | category | flops | bytes accessed | tf_op | source)
XLA Modules:
  0.0 72.1 jit_solution(10926259621866343655)
XLA Ops:
  0.6 1.3 %reshape.15.ln_ref = bf16[1,2048]{1,0:T(2,128)(2,1)} reshape(bf16[2048]{0:T(1024)(128)(2,1)} %param.15) | data formatting | bytes 8192 | tf_op jit(solution)/shard_map/reshape | solution.py:379
  1.9 65.5 %shard_map.139 = (bf16[64,2048]{1,0:T(8,128)(2,1)}, bf16[64,4,128]{2,1,0:T(4,128)(2,1)}, bf16[64,4,128]{2,1,0:T(4,128)(2,1)}) custom-call(bf16[64,2048]{1,0:T(8,128)(2,1)} %x_hbm.1, bf16[4096,4,128]{2,1,0:T(4,128)(2,1)} %k_hbm.1, bf16[4096,4,128]{2,1,0:T(4,128)(2,1)} %v_hbm.1, bf16[1,2048]{1,0:T(2,128)(2,1)} %reshape.15.ln_ref, bf16[2048,4096]{1,0:T(8,128)(2,1)} %wq_hbm.1, ...), custom_call_target="tpu_custom_call" | custom-call | tf_op jit(solution)/shard_map/pallas_call | solution.py:342
  67.4 1.7 %copy.18 = bf16[64,2048]{1,0:T(8,128)(2,1)} copy(bf16[64,2048]{1,0:T(8,128)(2,1)} %get-tuple-element.6) | data formatting | bytes 524288
  69.1 1.5 %copy.19 = bf16[64,4,128]{2,1,0:T(4,128)(2,1)} copy(bf16[64,4,128]{2,1,0:T(4,128)(2,1)} %get-tuple-element.7) | data formatting | bytes 131072
  70.6 1.5 %copy.20 = bf16[64,4,128]{2,1,0:T(4,128)(2,1)} copy(bf16[64,4,128]{2,1,0:T(4,128)(2,1)} %get-tuple-element.8) | data formatting | bytes 131072

commit v2 on v1

--- a/solution.py
+++ b/solution.py
@@ -27,7 +27,7 @@
 TILE = 256
 MSG = HEAD_DIM + 8
 HIDDEN = 2048
-CHUNK = 256
+CHUNK = 512
 
 
 def rope_tables(prefix_len):
@@ -38,11 +38,11 @@
     return np.cos(angles).astype(np.float32), np.sin(angles).astype(np.float32)
 
 
-def kernel(x_hbm, k_hbm, v_hbm, ln_ref, wq_hbm, wk_hbm, wv_hbm, wo_hbm, qg_ref, kg_ref, cos_ref, sin_ref,
+def kernel(x_hbm, k_hbm, v_hbm, ln_ref, wq_hbm, wk_hbm, wv_hbm, wo_hbm, qg_ref, kg_ref, cos_hbm, sin_hbm,
            out_ref, knew_ref, vnew_ref,
-           xall, hbuf, wbuf, wk, wv, kst, vst, kf, vf, ks, vt, qt, gq, gk, s_a, s_b, m_a, m_b,
+           cos_ref, sin_ref, xall, hbuf, wbuf, wk, wv, kst, vst, kf, vf, ks, vt, qt, gq, gk, s_a, s_b, m_a, m_b,
            abuf, bbuf, rbuf, cbuf, obuf,
-           x_sem, xs_sem, xr_sem, w_sem, kv_sem, cache_sem, wo_sem, as_sem, ar_sem, cs_sem, cr_sem):
+           x_sem, xs_sem, xr_sem, w_sem, kv_sem, tab_sem, cache_sem, wo_sem, as_sem, ar_sem, cs_sem, cr_sem):
     me = lax.axis_index("cp")
     dp = lax.axis_index("dp")
     partner = me + 1 - 2 * lax.rem(me, 2)
@@ -66,21 +66,21 @@
         kh = b % 2
         return pltpu.make_async_copy(wo_hbm.at[pl.ds(kh * 2048, 2048), pl.ds(nb * 512, 512)], wbuf.at[b], wo_sem.at[b])
 
-    NC = 4
-    CB = KEYS // NC
+    CB = KEYS // GROUPS
 
     def cache_copy(src, dst, j, n):
         return pltpu.make_async_copy(src.at[pl.ds(j * CB, CB)], dst.at[pl.ds(j * CB, CB)], cache_sem.at[n, j])
 
-    for g in range(4):
+    cos_copy = pltpu.make_async_copy(cos_hbm, cos_ref, tab_sem.at[0])
+    sin_copy = pltpu.make_async_copy(sin_hbm, sin_ref, tab_sem.at[1])
+    cos_copy.start()
+    sin_copy.start()
+    for g in range(GROUPS):
         wq_copy(g).start()
+        cache_copy(k_hbm, kst, g, 0).start()
+        cache_copy(v_hbm, vst, g, 1).start()
     wk_copy.start()
     wv_copy.start()
-    for g in range(4, GROUPS):
-        wq_copy(g).start()
-    for j in range(NC):
-        cache_copy(k_hbm, kst, j, 0).start()
-        cache_copy(v_hbm, vst, j, 1).start()
 
     barrier = pltpu.get_barrier_semaphore()
     for to in (partner, cross):
@@ -95,7 +95,7 @@
 
     gq[...] = jnp.broadcast_to(qg_ref[...].astype(F32), (HEAD_DIM, HEAD_DIM)).T
     gk[...] = jnp.broadcast_to(kg_ref[...].astype(F32), (HEAD_DIM, HEAD_DIM)).T
-    ln_gain = ln_ref[...].astype(F32)
+    ln_gain = ln_ref[...].astype(F32).reshape(1, HIDDEN)
 
     def normalise(slot):
         wide = xall[slot].astype(F32)
@@ -123,15 +123,27 @@
                 qt[units[n], :, hh * 128:(hh + 1) * 128] = norm_rope(two.T, gq[...], cos, sin)
 
     normalise(0)
+    cos_copy.wait()
+    sin_copy.wait()
     x_to_partner.wait_recv()
     normalise(1)
 
     def pair0(g, carry):
         wq_copy(g).wait()
+        cache_copy(k_hbm, kst, g, 0).wait()
+        cache_copy(v_hbm, vst, g, 1).wait()
         project(0, g)
+        at = pl.ds(pl.multiple_of(g * CHUNK, CHUNK), CHUNK)
+        kf[...] = kst[at].astype(F32).reshape(CHUNK * KV, HEAD_DIM)
+        vf[...] = vst[at].astype(F32).reshape(CHUNK * KV, HEAD_DIM)
+        for h in range(KV):
+            ks[h, at, :] = kf[pl.ds(h, CHUNK, stride=KV), :].astype(BF16)
+            vt[h, :, at] = vf[pl.ds(h, CHUNK, stride=KV), :].astype(BF16).T
         return carry
 
     lax.fori_loop(0, GROUPS, pair0, 0)
+    x_to_cross.wait_recv()
+    x_forward.start()
 
     wk_copy.wait()
     wv_copy.wait()
@@ -148,34 +160,12 @@
         vt[h, :, KEYS:ALL_KEYS] = one.T
         vnew_ref[:, h, :] = one
 
-    x_to_cross.wait_recv()
-    x_forward.start()
-    for j in range(NC):
-        cache_copy(k_hbm, kst, j, 0).wait()
-        cache_copy(v_hbm, vst, j, 1).wait()
-
-        def relayout(i, carry, j=j):
-            at = pl.ds(pl.multiple_of(j * CB + i * CHUNK, CHUNK), CHUNK)
-            kf[...] = kst[at].astype(F32).reshape(CHUNK * KV, HEAD_DIM)
-            vf[...] = vst[at].astype(F32).reshape(CHUNK * KV, HEAD_DIM)
-            for h in range(KV):
-                ks[h, at, :] = kf[pl.ds(h, CHUNK, stride=KV), :].astype(BF16)
-                vt[h, :, at] = vf[pl.ds(h, CHUNK, stride=KV), :].astype(BF16).T
-            return carry
-
-        lax.fori_loop(0, CB // CHUNK, relayout, 0)
-
     normalise(2)
     x_forward.wait_recv()
     normalise(3)
 
-    def pair1(g, carry):
-        project(1, g)
-        return carry
-
-    lax.fori_loop(0, GROUPS, pair1, 0)
-    for b in range(GROUPS):
-        wo_copy(b).start()
+    project(1, 0)
+    project(1, 1)
 
     tiles = [(t * TILE, TILE) for t in range(KEYS // TILE)] + [(KEYS, ROWS)]
 
@@ -258,7 +248,7 @@
         bbuf[g, 129:130, :] = total
         to_cross(g).start()
 
-    def attend(i, last):
+    def attend(i, last, ahead=False):
         a = begin(2 * i, s_a, m_a, None)
         b = begin(2 * i + 1, s_b, m_b, None)
         if not last:
@@ -270,6 +260,8 @@
                 weigh(z, t)
                 if not last:
                     score(z, t)
+            if ahead and t == 2:
+                project(1, i + 2)
         finish(a, abuf, i)
         finish(b, bbuf, i)
         if not last:
@@ -277,15 +269,18 @@
             end_next(b)
         to_partner(i).start()
 
-    def body(i, carry):
+    def body(ahead, i, carry):
         @pl.when(jnp.logical_and(i >= 2, i < GROUPS + 2))
         def _():
             combine_cross(i - 2)
 
-        attend(i, False)
+        attend(i, False, ahead)
         return carry
 
-    lax.fori_loop(0, 2 * GROUPS - 1, body, 0)
+    lax.fori_loop(0, GROUPS - 2, functools.partial(body, True), 0)
+    for b in range(GROUPS):
+        wo_copy(b).start()
+    lax.fori_loop(GROUPS - 2, 2 * GROUPS - 1, functools.partial(body, False), 0)
     attend(2 * GROUPS - 1, True)
 
     for g in range(GROUPS):
@@ -329,6 +324,11 @@
     lax.fori_loop(0, GROUPS, drain_cross, 0)
 
 
+def hand_over(*refs):
+    for src, dst in zip(refs[:3], refs[3:]):
+        dst[...] = src[...]
+
+
 def solution(mesh):
     row_spec = P(('dp', 'cp'), None)
     cache_spec = P(('dp', 'cp'), None, None)
@@ -339,15 +339,17 @@
     def device_step(x_rows, k_cache, v_cache, ln_gain, w_q, w_k, w_v, w_o, q_gain, k_gain):
         cos, sin = rope_tables(k_cache.shape[0] * CP)
         dma = pltpu.SemaphoreType.DMA
-        return pl.pallas_call(
+        results = pl.pallas_call(
             kernel,
             out_shape=(jax.ShapeDtypeStruct((ROWS, HIDDEN), BF16),
                        jax.ShapeDtypeStruct((ROWS, KV, HEAD_DIM), BF16),
                        jax.ShapeDtypeStruct((ROWS, KV, HEAD_DIM), BF16)),
             in_specs=[any_spec, any_spec, any_spec, vmem_spec, any_spec, any_spec, any_spec, any_spec,
-                      vmem_spec, vmem_spec, vmem_spec, vmem_spec],
+                      vmem_spec, vmem_spec, any_spec, any_spec],
             out_specs=(vmem_spec, vmem_spec, vmem_spec),
             scratch_shapes=[
+                pltpu.VMEM((CP, HALF, 128), F32),
+                pltpu.VMEM((CP, HALF, 128), F32),
                 pltpu.VMEM((4, ROWS, HIDDEN), BF16),
                 pltpu.VMEM((4 * ROWS, HIDDEN), BF16),
                 pltpu.VMEM((GROUPS, 2048, 512), BF16),
@@ -371,13 +373,16 @@
                 pltpu.VMEM((2 * GROUPS, MSG, COLS), F32),
                 pltpu.VMEM((GROUPS, MSG, COLS), F32),
                 pltpu.VMEM((ROWS, 4096), BF16),
-                dma, dma((3,)), dma((3,)), dma((GROUPS,)), dma((2,)), dma((2, 4)), dma((GROUPS,)),
+                dma, dma((3,)), dma((3,)), dma((GROUPS,)), dma((2,)), dma((2,)), dma((2, GROUPS)), dma((GROUPS,)),
                 dma((2 * GROUPS,)), dma((2 * GROUPS,)), dma((GROUPS,)), dma((GROUPS,)),
             ],
             compiler_params=pltpu.CompilerParams(collective_id=0, has_side_effects=True,
                                                  vmem_limit_bytes=67043328),
-        )(x_rows, k_cache, v_cache, ln_gain.reshape(1, -1), w_q, w_k, w_v, w_o,
+        )(x_rows, k_cache, v_cache, ln_gain, w_q, w_k, w_v, w_o,
           q_gain.reshape(1, -1), k_gain.reshape(1, -1), jnp.asarray(cos), jnp.asarray(sin))
+        return pl.pallas_call(
+            hand_over, out_shape=tuple(jax.ShapeDtypeStruct(r.shape, r.dtype) for r in results),
+            in_specs=[vmem_spec] * 3, out_specs=(vmem_spec,) * 3)(*results)
 
     return jax.shard_map(device_step, mesh=mesh,
                          in_specs=(row_spec, cache_spec, cache_spec, whole, whole, whole, whole, whole, whole, whole),

time: 72.3 us -> 63.6 us (0.88)
  local copies, waits for them, and re-layouts: 5.94 us -> 0 us
  Pallas kernels: 65.5 us -> 62.8 us
    unnamed x3 -> x0, local copies, waits for them, and re-layouts: 4.65 us -> none
    pallas_call x1, Pallas kernels: 65.5 us -> 61 us  [device_step(): pl.pallas_call(kernel, out_shape=(jax.ShapeDtypeStruct((ROWS, HIDDEN), BF...]
    pallas_call x0 -> x1, Pallas kernels: none -> 1.73 us  [device_step(): pl.pallas_call(hand_over, out_shape=tuple((jax.ShapeDtypeStruct(r.shape,...]
    reshape x1 -> x0, local copies, waits for them, and re-layouts: 1.29 us -> none  [device_step(): ln_gain.reshape(1, -1)]
where the time goes in v2:
time: 63.6 us; the launch traced here: 63.4 us
  Pallas kernels  62.8 us (99%)
  between operations  0.64 us (1%)
    pallas_call x1, Pallas kernels, device_step(): pl.pallas_call(kernel, out_shape=(jax.ShapeDtypeStruct((ROWS, HIDDEN), BF...  61 us
    pallas_call x1, Pallas kernels, device_step(): pl.pallas_call(hand_over, out_shape=tuple((jax.ShapeDtypeStruct(r.shape,...  1.73 us

profile of v2, /device:TPU:0, one launch (start us, length us, event | category | flops | bytes accessed | tf_op | source)
XLA Modules:
  0.0 63.4 jit_solution(12377574445505961739)
XLA Ops:
  0.6 61.0 %shard_map.139 = (bf16[64,2048]{1,0:T(8,128)(2,1)}, bf16[64,4,128]{2,1,0:T(4,128)(2,1)}, bf16[64,4,128]{2,1,0:T(4,128)(2,1)}) custom-call(bf16[64,2048]{1,0:T(8,128)(2,1)} %x_hbm.1, bf16[4096,4,128]{2,1,0:T(4,128)(2,1)} %k_hbm.1, bf16[4096,4,128]{2,1,0:T(4,128)(2,1)} %v_hbm.1, bf16[2048]{0:T(1024)(128)(2,1)} %ln_ref.1, bf16[2048,4096]{1,0:T(8,128)(2,1)} %wq_hbm.1, ...), custom_call_target="tpu_custom_call" | custom-call | tf_op jit(solution)/shard_map/pallas_call | solution.py:342
  61.7 1.7 %shard_map.140 = (bf16[64,2048]{1,0:T(8,128)(2,1)}, bf16[64,4,128]{2,1,0:T(4,128)(2,1)}, bf16[64,4,128]{2,1,0:T(4,128)(2,1)}) custom-call(bf16[64,2048]{1,0:T(8,128)(2,1)} %get-tuple-element.6.refs_0_, bf16[64,4,128]{2,1,0:T(4,128)(2,1)} %get-tuple-element.7.refs_1_, bf16[64,4,128]{2,1,0:T(4,128)(2,1)} %get-tuple-element.8.refs_2_), custom_call_target="tpu_custom_call" | custom-call | tf_op jit(solution)/shard_map/pallas_call | solution.py:383

commit v3 on v0

v3 whole, which is shorter than its diff:
```python
import functools

import jax
import jax.numpy as jnp
import numpy as np
from jax import lax
from jax.experimental import pallas as pl
from jax.experimental.pallas import tpu as pltpu
from jax.sharding import PartitionSpec as P

HEAD_DIM = 128
HALF = HEAD_DIM // 2
ROPE_THETA = 1.0e6
NORM_EPS = 1.0e-6
LOG2E = 1.4426950408889634
SCALE2 = HEAD_DIM ** -0.5 * LOG2E
MESH = pl.DeviceIdType.MESH
F32 = jnp.float32
BF16 = jnp.bfloat16
ROWS = 64
CP = 4
KEYS = 4096
ALL_KEYS = KEYS + ROWS
KV = 4
GROUPS = 8
COLS = 256
TILE = 256
MSG = HEAD_DIM + 8
HIDDEN = 2048
CHUNK = 512
FORWARD_AT = 4
EARLY = 8
VMEM_LIMIT = 60 * 1024 * 1024
EARLY_OUT = 6


def rope_tables(prefix_len):
    freq = (ROPE_THETA ** (-np.arange(HALF, dtype=np.float64) * (2.0 / HEAD_DIM))).astype(np.float32)
    pos = (prefix_len + np.arange(CP * ROWS)).astype(np.float32).reshape(CP, 1, ROWS)
    angles = (pos * freq[None, :, None]).astype(np.float32)
    angles = np.concatenate([angles, angles], axis=2).astype(np.float64)
    return np.cos(angles).astype(np.float32), np.sin(angles).astype(np.float32)


def kernel(x_hbm, k_hbm, v_hbm, ln_hbm, wq_hbm, wk_hbm, wv_hbm, wo_hbm, qg_hbm, kg_hbm, cos_hbm, sin_hbm,
           out_ref, knew_ref, vnew_ref,
           ln_ref, qg_ref, kg_ref, cos_ref, sin_ref, xall, hbuf, wbuf, ks, vt, qt, gq, gk, m_a, m_b,
           abuf, bbuf, rbuf, cbuf, obuf, part_out,
           x_sem, xs_sem, xr_sem, w_sem, kv_sem, tab_sem, cache_sem, wo_sem, as_sem, ar_sem, cs_sem, cr_sem):
    me = lax.axis_index("cp")
    dp = lax.axis_index("dp")
    partner = me + 1 - 2 * lax.rem(me, 2)
    cross = lax.rem(me + 2, CP)
    far = lax.rem(partner + 2, CP)

    def remote(src, dst, ssem, rsem, to):
        return pltpu.make_async_remote_copy(src_ref=src, dst_ref=dst, send_sem=ssem, recv_sem=rsem,
                                            device_id=(dp, to), device_id_type=MESH)

    x_copy = pltpu.make_async_copy(x_hbm, xall.at[0], x_sem)
    x_copy.start()
    small = [pltpu.make_async_copy(src, dst, tab_sem.at[n]) for n, (src, dst) in enumerate(
        ((ln_hbm, ln_ref), (qg_hbm, qg_ref), (kg_hbm, kg_ref), (cos_hbm, cos_ref), (sin_hbm, sin_ref)))]

    def wq_copy(g):
        return pltpu.make_async_copy(wq_hbm.at[:, pl.ds(pl.multiple_of(g * 512, 512), 512)], wbuf.at[g], w_sem.at[g])

    def wo_copy(b):
        nb = b // 2
        kh = b % 2
        return pltpu.make_async_copy(wo_hbm.at[pl.ds(kh * 2048, 2048), pl.ds(nb * 512, 512)], wbuf.at[b], wo_sem.at[b])

    x_to_cross = remote(xall.at[0], xall.at[2], xs_sem.at[1], xr_sem.at[1], cross)
    x_to_partner = remote(xall.at[0], xall.at[1], xs_sem.at[0], xr_sem.at[0], partner)
    x_forward = remote(xall.at[2], xall.at[3], xs_sem.at[2], xr_sem.at[2], partner)

    def normalise(slot):
        wide = xall[slot].astype(F32)
        mean_sq = jnp.mean(wide * wide, axis=-1, keepdims=True)
        ln_gain = ln_ref[...].astype(F32).reshape(1, HIDDEN)
        hbuf[slot * ROWS:(slot + 1) * ROWS, :] = (wide * lax.rsqrt(mean_sq + NORM_EPS) * ln_gain).astype(BF16)

    def norm_rope(raw_t, gain, cos, sin):
        z = raw_t.astype(F32)
        mean_sq = jnp.mean(z * z, axis=0, keepdims=True)
        y = z * lax.rsqrt(mean_sq + NORM_EPS) * gain
        first, second = y[:HALF], y[HALF:]
        return jnp.concatenate([first * cos - second * sin, second * cos + first * sin], axis=0).astype(BF16)

    def place(i):
        own = jnp.logical_or(i < 2, i >= GROUPS + 2)
        return jnp.where(i < 2, i, jnp.where(i < GROUPS + 2, i - 2, i - GROUPS)), own

    def project(i):
        g, own = place(i)
        ids = jnp.where(own, me, cross), jnp.where(own, partner, far)
        units = 2 * i + 1, 2 * i
        rows = pl.ds(pl.multiple_of(jnp.where(own, 0, 2 * ROWS), 2 * ROWS), 2 * ROWS)
        raw = jnp.dot(hbuf[rows, :], wbuf[g], preferred_element_type=F32).astype(BF16)
        for n in range(2):
            cos, sin = cos_ref[ids[n]], sin_ref[ids[n]]
            part = raw[n * ROWS:(n + 1) * ROWS]
            for hh in range(2):
                two = jnp.concatenate([part[:, hh * 256:hh * 256 + 128], part[:, hh * 256 + 128:hh * 256 + 256]], axis=0)
                qt[units[n], :, hh * 128:(hh + 1) * 128] = norm_rope(two.T, gq[...], cos, sin)

    def prologue(wk, wv, kst, vst, kf, vf):
        def cache_copy(src, dst, j, n):
            at = pl.ds(pl.multiple_of(j * CHUNK * KV, CHUNK * KV), CHUNK * KV)
            return pltpu.make_async_copy(src.at[at], dst.at[at], cache_sem.at[n, j])

        wk_copy = pltpu.make_async_copy(wk_hbm, wk, kv_sem.at[0])
        wv_copy = pltpu.make_async_copy(wv_hbm, wv, kv_sem.at[1])
        for j in range(EARLY):
            cache_copy(k_hbm, kst, j, 0).start()
            cache_copy(v_hbm, vst, j, 1).start()

        barrier = pltpu.get_barrier_semaphore()
        for to in (partner, cross):
            pl.semaphore_signal(barrier, inc=1, device_id=(dp, to), device_id_type=MESH)
        pl.semaphore_wait(barrier, 2)
        x_copy.wait()
        x_to_cross.start()
        x_to_partner.start()
        for c in small:
            c.start()
        for j in range(EARLY, GROUPS):
            cache_copy(k_hbm, kst, j, 0).start()
            cache_copy(v_hbm, vst, j, 1).start()
        wk_copy.start()
        wv_copy.start()
        for g in range(GROUPS):
            wq_copy(g).start()

        def relayout(j, carry):
            cache_copy(k_hbm, kst, j, 0).wait()
            cache_copy(v_hbm, vst, j, 1).wait()
            at = pl.ds(pl.multiple_of(j * CHUNK * KV, CHUNK * KV), CHUNK * KV)
            to = pl.ds(pl.multiple_of(j * CHUNK, CHUNK), CHUNK)
            kf[...] = kst[at].astype(F32)
            vf[...] = vst[at].astype(F32)
            for h in range(KV):
                ks[h, to, :] = kf[pl.ds(h, CHUNK, stride=KV), :].astype(BF16)
                vt[h, :, to] = vf[pl.ds(h, CHUNK, stride=KV), :].astype(BF16).T
            return carry

        lax.fori_loop(0, GROUPS, relayout, 0)

        for c in small:
            c.wait()
        gq[...] = jnp.broadcast_to(qg_ref[...].astype(F32), (HEAD_DIM, HEAD_DIM)).T
        gk[...] = jnp.broadcast_to(kg_ref[...].astype(F32), (HEAD_DIM, HEAD_DIM)).T
        normalise(0)
        x_to_partner.wait_recv()
        normalise(1)

        wk_copy.wait()
        wv_copy.wait()
        k_raw = jnp.dot(hbuf[0:ROWS, :], wk[...], preferred_element_type=F32).astype(BF16)
        v_raw = jnp.dot(hbuf[0:ROWS, :], wv[...], preferred_element_type=F32).astype(BF16)
        for hh in range(2):
            two = jnp.concatenate([k_raw[:, hh * 256:hh * 256 + 128], k_raw[:, hh * 256 + 128:hh * 256 + 256]], axis=0)
            back = norm_rope(two.T, gk[...], cos_ref[me], sin_ref[me]).T
            for n in range(2):
                ks[2 * hh + n, KEYS:ALL_KEYS, :] = back[n * ROWS:(n + 1) * ROWS]
                knew_ref[:, 2 * hh + n, :] = back[n * ROWS:(n + 1) * ROWS]
        for h in range(KV):
            one = v_raw[:, h * 128:(h + 1) * 128]
            vt[h, :, KEYS:ALL_KEYS] = one.T
            vnew_ref[:, h, :] = one

    def main(s_a, s_b):
        for g in range(2):
            wq_copy(g).wait()
            project(g)

        tiles = [(t * TILE, TILE) for t in range(KEYS // TILE)] + [(KEYS, ROWS)]

        def colmax(s, n):
            return jnp.max(s.reshape(n // 8, 8, COLS), axis=0)

        class Unit:
            pass

        def begin(u, s_ref, m_ref, dest):
            z = Unit()
            z.s, z.m = s_ref, m_ref
            z.peak = m_ref[0:1]
            z.head = place(u // 2)[0] // 2
            z.acc = z.sum = None
            return z

        def begin_next(z, u, s_ref, m_ref, dest):
            z.s, z.m = s_ref, m_ref
            z.next_head = place(u // 2)[0] // 2
            z.q = qt[u]
            z.dest = dest
            z.top = None
            return z

        def weigh(z, t):
            lo, n = tiles[t]
            p = jnp.exp2(z.s[lo:lo + n, :] * SCALE2 - z.peak)
            part = jnp.sum(p.reshape(n // 8, 8, COLS), axis=0)
            z.sum = part if z.sum is None else z.sum + part
            a = jnp.dot(vt[z.head, :, lo:lo + n], p.astype(BF16), preferred_element_type=F32)
            z.acc = a if z.acc is None else z.acc + a

        def score(z, t):
            lo, n = tiles[t]
            s = jnp.dot(ks[z.next_head, lo:lo + n, :], z.q, preferred_element_type=F32)
            if t == len(tiles) - 1:
                key = me * ROWS + lax.broadcasted_iota(jnp.int32, (n, COLS), 0)
                row = z.dest * ROWS + (lax.broadcasted_iota(jnp.int32, (n, COLS), 1) & (ROWS - 1))
                s = jnp.where(key <= row, s, -jnp.inf)
            z.s[lo:lo + n, :] = s
            top = colmax(s, n)
            z.top = top if z.top is None else jnp.maximum(z.top, top)

        def end_next(z):
            z.m[0:1] = jnp.max(z.top, axis=0, keepdims=True) * SCALE2

        def finish(z, ref, slot):
            ref[slot, 0:HEAD_DIM, :] = z.acc
            ref[slot, HEAD_DIM:HEAD_DIM + 1, :] = z.peak
            ref[slot, HEAD_DIM + 1:HEAD_DIM + 2, :] = jnp.sum(z.sum, axis=0, keepdims=True)

        def dests(i):
            own = place(i)[1]
            return jnp.where(own, partner, far), jnp.where(own, me, cross)

        za, zb = Unit(), Unit()
        da, db = partner, me
        begin_next(za, 0, s_a, m_a, da)
        begin_next(zb, 1, s_b, m_b, db)
        for t in range(len(tiles)):
            score(za, t)
            score(zb, t)
        end_next(za)
        end_next(zb)

        def to_partner(i):
            return remote(abuf.at[i], rbuf.at[i], as_sem.at[i], ar_sem.at[i], partner)

        def to_cross(g):
            return remote(bbuf.at[g + 2], cbuf.at[g], cs_sem.at[g], cr_sem.at[g], cross)

        def combine_cross(g):
            n = g + 2
            to_partner(n).wait_recv()
            m1, m2 = bbuf[n, 128:129, :], rbuf[n, 128:129, :]
            m = jnp.maximum(m1, m2)
            w1, w2 = jnp.exp2(m1 - m), jnp.exp2(m2 - m)
            bbuf[n, 0:128, :] = bbuf[n, 0:128, :] * w1 + rbuf[n, 0:128, :] * w2
            total = bbuf[n, 129:130, :] * w1 + rbuf[n, 129:130, :] * w2
            bbuf[n, 128:129, :] = m
            bbuf[n, 129:130, :] = total
            to_cross(g).start()

        def attend(i, last, ahead=False, beside=None):
            a = begin(2 * i, s_a, m_a, None)
            b = begin(2 * i + 1, s_b, m_b, None)
            if not last:
                da, db = dests(i + 1)
                begin_next(a, 2 * i + 2, s_a, m_a, da)
                begin_next(b, 2 * i + 3, s_b, m_b, db)
            for t in range(len(tiles)):
                for z in (a, b):
                    weigh(z, t)
                    if not last:
                        score(z, t)
                if ahead and t == 2:
                    project(i + 2)
                if beside is not None:
                    beside(t)
            finish(a, abuf, i)
            finish(b, bbuf, i)
            if not last:
                end_next(a)
                end_next(b)
            to_partner(i).start()

        def forward(t):
            if t == FORWARD_AT:
                x_to_cross.wait_recv()
                x_forward.start()

        def body(i, carry):
            @pl.when(jnp.logical_and(i >= 4, i < GROUPS + 4))
            def _():
                combine_cross(i - 4)

            @pl.when(jnp.logical_or(i == 2, i == 3))
            def _():
                wo_copy(i - 2).start()

            @pl.when(i >= GROUPS + 1)
            def _():
                wo_copy(i - GROUPS + 1).start()

            @pl.when(jnp.logical_and(i >= 2, i < GROUPS))
            def _():
                wq_copy(i).wait()

            attend(i, False, True)
            return carry

        attend(0, False, beside=forward)
        normalise(2)
        x_forward.wait_recv()
        normalise(3)
        project(2)
        lax.fori_loop(1, 2 * GROUPS - 2, body, 0)
        wo_copy(GROUPS - 1).start()
        attend(2 * GROUPS - 2, False)

        def slot_of(g):
            return g if g < 2 else GROUPS + g

        def arrive(g):
            to_partner(slot_of(g)).wait_recv()
            to_cross(g).wait_recv()

        def finish_group(g):
            parts = ((bbuf, slot_of(g)), (rbuf, slot_of(g)), (cbuf, g))
            peaks = [ref[n, 128:129, :] for ref, n in parts]
            m = jnp.maximum(jnp.maximum(peaks[0], peaks[1]), peaks[2])
            ws = [jnp.exp2(p - m) for p in peaks]
            total = sum(ref[n, 129:130, :] * w for (ref, n), w in zip(parts, ws))
            inv = 1.0 / total
            o = sum(ref[n, 0:128, :] * (w * inv) for (ref, n), w in zip(parts, ws)).astype(BF16)
            for hh in range(2):
                rows = o[:, hh * 128:(hh + 1) * 128].T
                for n in range(2):
                    col = (4 * g + 2 * hh + n) * HEAD_DIM
                    obuf[:, col:col + HEAD_DIM] = rows[n * ROWS:(n + 1) * ROWS]

        split = EARLY_OUT * 512

        def project_early(nb):
            cols = slice(nb * 512, (nb + 1) * 512)
            acc = jnp.dot(obuf[:, 0:2048], wbuf[2 * nb], preferred_element_type=F32)
            acc = acc + jnp.dot(obuf[:, 2048:split], wbuf[2 * nb + 1, 0:split - 2048], preferred_element_type=F32)
            part_out[:, cols] = acc

        def beside(t):
            if t < EARLY_OUT:
                finish_group(t)
            elif t in (7, 9, 11, 13):
                project_early((t - 7) // 2)

        for g in range(EARLY_OUT):
            arrive(g)
        for b in range(GROUPS):
            wo_copy(b).wait()
        attend(2 * GROUPS - 1, True, beside=beside)
        for g in range(EARLY_OUT, GROUPS):
            arrive(g)
        for g in range(EARLY_OUT, GROUPS):
            finish_group(g)
        for nb in range(4):
            cols = slice(nb * 512, (nb + 1) * 512)
            acc = jnp.dot(obuf[:, split:4096], wbuf[2 * nb + 1, split - 2048:2048], preferred_element_type=F32)
            out_ref[:, cols] = (xall[0, :, cols].astype(F32) + (part_out[:, cols] + acc)).astype(BF16)

        x_to_partner.wait_send()
        x_to_cross.wait_send()
        x_forward.wait_send()

        def drain(i, carry):
            to_partner(i).wait_send()
            return carry

        lax.fori_loop(0, 2 * GROUPS, drain, 0)

        def drain_cross(g, carry):
            to_cross(g).wait_send()
            return carry

        lax.fori_loop(0, GROUPS, drain_cross, 0)

    pl.run_scoped(
        prologue,
        pltpu.VMEM((HIDDEN, 512), BF16),
        pltpu.VMEM((HIDDEN, 512), BF16),
        pltpu.VMEM((KEYS * KV, HEAD_DIM), BF16),
        pltpu.VMEM((KEYS * KV, HEAD_DIM), BF16),
        pltpu.VMEM((CHUNK * KV, HEAD_DIM), F32),
        pltpu.VMEM((CHUNK * KV, HEAD_DIM), F32),
    )
    pl.run_scoped(main, pltpu.VMEM((ALL_KEYS, COLS), F32), pltpu.VMEM((ALL_KEYS, COLS), F32))

def hand_over(*refs):
    for src, dst in zip(refs[:3], refs[3:]):
        dst[...] = src[...]


def solution(mesh):
    row_spec = P(('dp', 'cp'), None)
    cache_spec = P(('dp', 'cp'), None, None)
    whole = P()
    any_spec = pl.BlockSpec(memory_space=pl.ANY)
    vmem_spec = pl.BlockSpec(memory_space=pltpu.VMEM)

    def device_step(x_rows, k_cache, v_cache, ln_gain, w_q, w_k, w_v, w_o, q_gain, k_gain):
        cos, sin = rope_tables(k_cache.shape[0] * CP)
        dma = pltpu.SemaphoreType.DMA
        results = pl.pallas_call(
            kernel,
            out_shape=(jax.ShapeDtypeStruct((ROWS, HIDDEN), BF16),
                       jax.ShapeDtypeStruct((ROWS, KV, HEAD_DIM), BF16),
                       jax.ShapeDtypeStruct((ROWS, KV, HEAD_DIM), BF16)),
            in_specs=[any_spec] * 12,
            out_specs=(vmem_spec, vmem_spec, vmem_spec),
            scratch_shapes=[
                pltpu.VMEM((HIDDEN,), BF16),
                pltpu.VMEM((1, HEAD_DIM), BF16),
                pltpu.VMEM((1, HEAD_DIM), BF16),
                pltpu.VMEM((CP, HALF, 128), F32),
                pltpu.VMEM((CP, HALF, 128), F32),
                pltpu.VMEM((4, ROWS, HIDDEN), BF16),
                pltpu.VMEM((4 * ROWS, HIDDEN), BF16),
                pltpu.VMEM((GROUPS, 2048, 512), BF16),
                pltpu.VMEM((KV, ALL_KEYS, HEAD_DIM), BF16),
                pltpu.VMEM((KV, HEAD_DIM, ALL_KEYS), BF16),
                pltpu.VMEM((4 * GROUPS, HEAD_DIM, COLS), BF16),
                pltpu.VMEM((HEAD_DIM, HEAD_DIM), F32),
                pltpu.VMEM((HEAD_DIM, HEAD_DIM), F32),
                pltpu.VMEM((8, COLS), F32),
                pltpu.VMEM((8, COLS), F32),
                pltpu.VMEM((2 * GROUPS, MSG, COLS), F32),
                pltpu.VMEM((2 * GROUPS, MSG, COLS), F32),
                pltpu.VMEM((2 * GROUPS, MSG, COLS), F32),
                pltpu.VMEM((GROUPS, MSG, COLS), F32),
                pltpu.VMEM((ROWS, 4096), BF16),
                pltpu.VMEM((ROWS, HIDDEN), F32),
                dma, dma((3,)), dma((3,)), dma((GROUPS,)), dma((2,)), dma((5,)), dma((2, GROUPS)), dma((GROUPS,)),
                dma((2 * GROUPS,)), dma((2 * GROUPS,)), dma((GROUPS,)), dma((GROUPS,)),
            ],
            compiler_params=pltpu.CompilerParams(collective_id=0, has_side_effects=True,
                                                 vmem_limit_bytes=VMEM_LIMIT),
        )(x_rows, k_cache.reshape(-1, HEAD_DIM), v_cache.reshape(-1, HEAD_DIM), ln_gain, w_q, w_k, w_v, w_o,
          q_gain.reshape(1, -1), k_gain.reshape(1, -1), jnp.asarray(cos), jnp.asarray(sin))
        return pl.pallas_call(
            hand_over, out_shape=tuple(jax.ShapeDtypeStruct(r.shape, r.dtype) for r in results),
            in_specs=[vmem_spec] * 3, out_specs=(vmem_spec,) * 3)(*results)

    return jax.shard_map(device_step, mesh=mesh,
                         in_specs=(row_spec, cache_spec, cache_spec, whole, whole, whole, whole, whole, whole, whole),
                         out_specs=(row_spec, cache_spec, cache_spec), check_vma=False)
```

time: 339 us -> 57.4 us (0.17)
  matrix products: 149 us -> 0 us
  other arithmetic: 70.4 us -> 0 us
  Pallas kernels: 0 us -> 56.6 us
  waiting for transfers between devices: 43.3 us -> 0 us
  blocking collectives: 25.8 us -> 0 us
  local copies, waits for them, and re-layouts: 23.7 us -> 0 us
  between operations: 14.5 us -> 0.64 us
  starting transfers between devices: 8.52 us -> 0 us
    dot_general x20 -> x0, matrix products: 149 us -> none  [the longest x8 66 us: partial_attend(): jnp.einsum('krgs,skd->krgd', weights.astype(jnp.bfloat16), vals, preferre...]
    reduce_sum x10 -> x0, other arithmetic: 63.6 us -> none  [the longest x4 56.1 us: partial_attend(): return (peak, jnp.sum(weights, axis=-1), weighted)]
    pallas_call x0 -> x2, Pallas kernels: none -> 56.6 us  [the longest x1 54.9 us: device_step(): pl.pallas_call(kernel, out_shape=(jax.ShapeDtypeStruct((ROWS, HIDDEN), BF...]
    all_to_all x2 -> x0, waiting for transfers between devices: 43.3 us -> none  [device_step(): lax.all_to_all(piece, 'cp', 0, 0, tiled=True)]
    all_gather x2 -> x0, blocking collectives: 19.5 us -> none  [the longest x1 11.5 us: device_step(): every_k = lax.all_gather(k_new, 'cp')]
    unnamed x38 -> x0, local copies, waits for them, and re-layouts: 11 us -> none
    all_to_all x2 -> x0, starting transfers between devices: 8.48 us -> none  [device_step(): lax.all_to_all(piece, 'cp', 0, 0, tiled=True)]
    all_to_all x1 -> x0, blocking collectives: 6.29 us -> none  [device_step(): lax.all_to_all(piece, 'cp', 0, 0, tiled=True)]
  transfers between devices with their start and end apart: 3 -> 0, of which waited for: 2 -> 0; matrix products, arithmetic and copies ran while one was open for 6% -> 0% of each run, Pallas kernels for 0% -> 0%
where the time goes in v3:
time: 57.4 us; the launch traced here: 57.3 us
  Pallas kernels  56.6 us (99%)
  between operations  0.64 us (1%)
    pallas_call x1, Pallas kernels, device_step(): pl.pallas_call(kernel, out_shape=(jax.ShapeDtypeStruct((ROWS, HIDDEN), BF...  54.9 us
    pallas_call x1, Pallas kernels, device_step(): pl.pallas_call(hand_over, out_shape=tuple((jax.ShapeDtypeStruct(r.shape,...  1.73 us

profile of v3, /device:TPU:0, one launch (start us, length us, event | category | flops | bytes accessed | tf_op | source)
XLA Modules:
  0.0 57.3 jit_solution(15932583707918048403)
XLA Ops:
  0.6 54.9 %shard_map.139 = (bf16[64,2048]{1,0:T(8,128)(2,1)}, bf16[64,4,128]{2,1,0:T(4,128)(2,1)}, bf16[64,4,128]{2,1,0:T(4,128)(2,1)}) custom-call(bf16[64,2048]{1,0:T(8,128)(2,1)} %x_hbm.1, bf16[16384,128]{1,0:T(8,128)(2,1)} %bitcast.4, bf16[16384,128]{1,0:T(8,128)(2,1)} %bitcast.5, bf16[2048]{0:T(1024)(128)(2,1)} %ln_hbm.1, bf16[2048,4096]{1,0:T(8,128)(2,1)} %wq_hbm.1, ...), custom_call_target="tpu_custom_call" | custom-call | tf_op jit(solution)/shard_map/pallas_call | solution.py:408
  55.5 1.7 %shard_map.140 = (bf16[64,2048]{1,0:T(8,128)(2,1)}, bf16[64,4,128]{2,1,0:T(4,128)(2,1)}, bf16[64,4,128]{2,1,0:T(4,128)(2,1)}) custom-call(bf16[64,2048]{1,0:T(8,128)(2,1)} %get-tuple-element.6.refs_0_, bf16[64,4,128]{2,1,0:T(4,128)(2,1)} %get-tuple-element.7.refs_1_, bf16[64,4,128]{2,1,0:T(4,128)(2,1)} %get-tuple-element.8.refs_2_), custom_call_target="tpu_custom_call" | custom-call | tf_op jit(solution)/shard_map/pallas_call | solution.py:444

commit v4 on v3

--- a/solution.py
+++ b/solution.py
@@ -28,9 +28,10 @@
 MSG = HEAD_DIM + 8
 HIDDEN = 2048
 CHUNK = 512
-FORWARD_AT = 4
+FORWARD_AT = 2
 EARLY = 8
 VMEM_LIMIT = 60 * 1024 * 1024
+SHARED = 6
 EARLY_OUT = 6
 
 
@@ -46,10 +47,11 @@
            out_ref, knew_ref, vnew_ref,
            ln_ref, qg_ref, kg_ref, cos_ref, sin_ref, xall, hbuf, wbuf, ks, vt, qt, gq, gk, m_a, m_b,
            abuf, bbuf, rbuf, cbuf, obuf, part_out,
-           x_sem, xs_sem, xr_sem, w_sem, kv_sem, tab_sem, cache_sem, wo_sem, as_sem, ar_sem, cs_sem, cr_sem):
+           x_sem, xs_sem, xr_sem, w_sem, kv_sem, tab_sem, cache_sem, wo_sem, as_sem, ar_sem, cs_sem, cr_sem, qs_sem, qr_sem):
     me = lax.axis_index("cp")
     dp = lax.axis_index("dp")
-    partner = me + 1 - 2 * lax.rem(me, 2)
+    core = lax.rem(me, 2)
+    partner = me + 1 - 2 * core
     cross = lax.rem(me + 2, CP)
     far = lax.rem(partner + 2, CP)
 
@@ -129,8 +131,12 @@
             cache_copy(v_hbm, vst, j, 1).start()
         wk_copy.start()
         wv_copy.start()
-        for g in range(GROUPS):
+        for g in range(2):
             wq_copy(g).start()
+        for m in range(1, 4):
+            wq_copy(2 * m + core).start()
+        for m in range(1, 4):
+            wo_copy(2 * m + 1 - core).start()
 
         def relayout(j, carry):
             cache_copy(k_hbm, kst, j, 0).wait()
@@ -257,7 +263,15 @@
             bbuf[n, 129:130, :] = total
             to_cross(g).start()
 
-        def attend(i, last, ahead=False, beside=None):
+        def shared_place(m, c):
+            return 4 + 2 * m + c
+
+        def share(m, c):
+            p = shared_place(m, c)
+            return [remote(qt.at[2 * p + n], qt.at[2 * p + 1 - n], qs_sem.at[m, n], qr_sem.at[m, n], partner)
+                    for n in range(2)]
+
+        def attend(i, last, ahead=(), beside=None):
             a = begin(2 * i, s_a, m_a, None)
             b = begin(2 * i + 1, s_b, m_b, None)
             if not last:
@@ -269,8 +283,9 @@
                     weigh(z, t)
                     if not last:
                         score(z, t)
-                if ahead and t == 2:
-                    project(i + 2)
+                for n, p in enumerate(ahead):
+                    if t == 2 + 5 * n:
+                        project(p)
                 if beside is not None:
                     beside(t)
             finish(a, abuf, i)
@@ -285,24 +300,48 @@
                 x_to_cross.wait_recv()
                 x_forward.start()
 
-        def body(i, carry):
+        def before(i):
             @pl.when(jnp.logical_and(i >= 4, i < GROUPS + 4))
             def _():
                 combine_cross(i - 4)
 
-            @pl.when(jnp.logical_or(i == 2, i == 3))
+        def body(n, carry):
+            i = 2 + 2 * n
+            before(i)
+
+            @pl.when(n == 0)
             def _():
-                wo_copy(i - 2).start()
-
-            @pl.when(i >= GROUPS + 1)
+                wo_copy(0).start()
+                wo_copy(1).start()
+
+            attend(i, False)
+            before(i + 1)
+            for c in share(n, 1 - core):
+                c.wait_recv()
+
+            @pl.when(n < 2)
             def _():
-                wo_copy(i - GROUPS + 1).start()
-
-            @pl.when(jnp.logical_and(i >= 2, i < GROUPS))
+                wq_copy(2 * (n + 2) + core).wait()
+
+            attend(i + 1, False, ahead=(shared_place(n + 1, core),))
+            for c in share(n + 1, core):
+                c.start()
+
+            @pl.when(n >= 2)
             def _():
-                wq_copy(i).wait()
-
-            attend(i, False, True)
+                wo_copy(2 * (n - 1) + core).start()
+
+            return carry
+
+        def late_body(i, carry):
+            before(i)
+
+            @pl.when(i == 2 * GROUPS - 3)
+            def _():
+                for c in share(SHARED - 1, 1 - core):
+                    c.wait_recv()
+
+            attend(i, False)
             return carry
 
         attend(0, False, beside=forward)
@@ -310,9 +349,12 @@
         x_forward.wait_recv()
         normalise(3)
         project(2)
-        lax.fori_loop(1, 2 * GROUPS - 2, body, 0)
-        wo_copy(GROUPS - 1).start()
-        attend(2 * GROUPS - 2, False)
+        wq_copy(2 + core).wait()
+        attend(1, False, ahead=(3, shared_place(0, core)))
+        for c in share(0, core):
+            c.start()
+        lax.fori_loop(0, 5, body, 0)
+        lax.fori_loop(12, 15, late_body, 0)
 
         def slot_of(g):
             return g if g < 2 else GROUPS + g
@@ -366,6 +408,9 @@
         x_to_partner.wait_send()
         x_to_cross.wait_send()
         x_forward.wait_send()
+        for m in range(SHARED):
+            for c in share(m, core):
+                c.wait_send()
 
         def drain(i, carry):
             to_partner(i).wait_send()
@@ -436,6 +481,7 @@
                 pltpu.VMEM((ROWS, HIDDEN), F32),
                 dma, dma((3,)), dma((3,)), dma((GROUPS,)), dma((2,)), dma((5,)), dma((2, GROUPS)), dma((GROUPS,)),
                 dma((2 * GROUPS,)), dma((2 * GROUPS,)), dma((GROUPS,)), dma((GROUPS,)),
+                dma((SHARED, 2)), dma((SHARED, 2)),
             ],
             compiler_params=pltpu.CompilerParams(collective_id=0, has_side_effects=True,
                                                  vmem_limit_bytes=VMEM_LIMIT),

time: 57.4 us -> 55.6 us (0.969)
  Pallas kernels: 56.6 us -> 54.8 us
    pallas_call x1, Pallas kernels: 54.9 us -> 53.1 us  [device_step(): pl.pallas_call(kernel, out_shape=(jax.ShapeDtypeStruct((ROWS, HIDDEN), BF...]
where the time goes in v4:
time: 55.6 us; the launch traced here: 55.4 us
  Pallas kernels  54.8 us (99%)
  between operations  0.64 us (1%)
    pallas_call x1, Pallas kernels, device_step(): pl.pallas_call(kernel, out_shape=(jax.ShapeDtypeStruct((ROWS, HIDDEN), BF...  53.1 us
    pallas_call x1, Pallas kernels, device_step(): pl.pallas_call(hand_over, out_shape=tuple((jax.ShapeDtypeStruct(r.shape,...  1.73 us

profile of v4, /device:TPU:0, one launch (start us, length us, event | category | flops | bytes accessed | tf_op | source)
XLA Modules:
  0.0 55.4 jit_solution(4692224490393018186)
XLA Ops:
  0.6 53.1 %shard_map.139 = (bf16[64,2048]{1,0:T(8,128)(2,1)}, bf16[64,4,128]{2,1,0:T(4,128)(2,1)}, bf16[64,4,128]{2,1,0:T(4,128)(2,1)}) custom-call(bf16[64,2048]{1,0:T(8,128)(2,1)} %x_hbm.1, bf16[16384,128]{1,0:T(8,128)(2,1)} %bitcast.4, bf16[16384,128]{1,0:T(8,128)(2,1)} %bitcast.5, bf16[2048]{0:T(1024)(128)(2,1)} %ln_hbm.1, bf16[2048,4096]{1,0:T(8,128)(2,1)} %wq_hbm.1, ...), custom_call_target="tpu_custom_call" | custom-call | tf_op jit(solution)/shard_map/pallas_call | solution.py:453
  53.7 1.7 %shard_map.140 = (bf16[64,2048]{1,0:T(8,128)(2,1)}, bf16[64,4,128]{2,1,0:T(4,128)(2,1)}, bf16[64,4,128]{2,1,0:T(4,128)(2,1)}) custom-call(bf16[64,2048]{1,0:T(8,128)(2,1)} %get-tuple-element.6.refs_0_, bf16[64,4,128]{2,1,0:T(4,128)(2,1)} %get-tuple-element.7.refs_1_, bf16[64,4,128]{2,1,0:T(4,128)(2,1)} %get-tuple-element.8.refs_2_), custom_call_target="tpu_custom_call" | custom-call | tf_op jit(solution)/shard_map/pallas_call | solution.py:490

commit v5 on v4

--- a/solution.py
+++ b/solution.py
@@ -452,9 +452,9 @@
         dma = pltpu.SemaphoreType.DMA
         results = pl.pallas_call(
             kernel,
-            out_shape=(jax.ShapeDtypeStruct((ROWS, HIDDEN), BF16),
-                       jax.ShapeDtypeStruct((ROWS, KV, HEAD_DIM), BF16),
-                       jax.ShapeDtypeStruct((ROWS, KV, HEAD_DIM), BF16)),
+            out_shape=(pltpu.VMEM((ROWS, HIDDEN), BF16),
+                       pltpu.VMEM((ROWS, KV, HEAD_DIM), BF16),
+                       pltpu.VMEM((ROWS, KV, HEAD_DIM), BF16)),
             in_specs=[any_spec] * 12,
             out_specs=(vmem_spec, vmem_spec, vmem_spec),
             scratch_shapes=[
@@ -489,7 +489,8 @@
           q_gain.reshape(1, -1), k_gain.reshape(1, -1), jnp.asarray(cos), jnp.asarray(sin))
         return pl.pallas_call(
             hand_over, out_shape=tuple(jax.ShapeDtypeStruct(r.shape, r.dtype) for r in results),
-            in_specs=[vmem_spec] * 3, out_specs=(vmem_spec,) * 3)(*results)
+            in_specs=[vmem_spec] * 3, out_specs=(vmem_spec,) * 3,
+        )(*[pltpu.with_memory_space_constraint(r, pltpu.VMEM) for r in results])
 
     return jax.shard_map(device_step, mesh=mesh,
                          in_specs=(row_spec, cache_spec, cache_spec, whole, whole, whole, whole, whole, whole, whole),

time: 55.6 us -> 53.8 us (0.968)
  Pallas kernels: 54.8 us -> 53.1 us
    pallas_call x1, Pallas kernels: 1.73 us -> 0.76 us  [device_step(): pl.pallas_call(hand_over, out_shape=tuple((jax.ShapeDtypeStruct(r.shape,...]
    pallas_call x1, Pallas kernels: 53.1 us -> 52.3 us  [device_step(): pl.pallas_call(kernel, out_shape=(pltpu.VMEM((ROWS, HIDDEN), BF16), pltpu...]
where the time goes in v5:
time: 53.8 us; the launch traced here: 53.7 us
  Pallas kernels  53.1 us (99%)
  between operations  0.64 us (1%)
    pallas_call x1, Pallas kernels, device_step(): pl.pallas_call(kernel, out_shape=(pltpu.VMEM((ROWS, HIDDEN), BF16), pltpu...  52.3 us

profile of v5, /device:TPU:0, one launch (start us, length us, event | category | flops | bytes accessed | tf_op | source)
XLA Modules:
  0.0 53.7 jit_solution(8121524966993978601)
XLA Ops:
  0.6 52.3 %shard_map.139 = (bf16[64,2048]{1,0:T(8,128)(2,1)S(1)}, bf16[64,4,128]{2,1,0:T(4,128)(2,1)S(1)}, bf16[64,4,128]{2,1,0:T(4,128)(2,1)S(1)}) custom-call(bf16[64,2048]{1,0:T(8,128)(2,1)} %x_hbm.1, bf16[16384,128]{1,0:T(8,128)(2,1)} %bitcast.4, bf16[16384,128]{1,0:T(8,128)(2,1)} %bitcast.5, bf16[2048]{0:T(1024)(128)(2,1)} %ln_hbm.1, bf16[2048,4096]{1,0:T(8,128)(2,1)} %wq_hbm.1, ...), custom_call_target="tpu_custom_call" | custom-call | tf_op jit(solution)/shard_map/pallas_call | solution.py:453
  52.9 0.8 %shard_map.140 = (bf16[64,2048]{1,0:T(8,128)(2,1)}, bf16[64,4,128]{2,1,0:T(4,128)(2,1)}, bf16[64,4,128]{2,1,0:T(4,128)(2,1)}) custom-call(bf16[64,2048]{1,0:T(8,128)(2,1)S(1)} %get-tuple-element.6.refs_0_, bf16[64,4,128]{2,1,0:T(4,128)(2,1)S(1)} %get-tuple-element.7.refs_1_, bf16[64,4,128]{2,1,0:T(4,128)(2,1)S(1)} %get-tuple-element.8.refs_2_), custom_call_target="tpu_custom_call" | custom-call | tf_op jit(solution)/shard_map/pallas_call | solution.py:490

commit v6 on v5

--- a/solution.py
+++ b/solution.py
@@ -253,7 +253,6 @@
 
         def combine_cross(g):
             n = g + 2
-            to_partner(n).wait_recv()
             m1, m2 = bbuf[n, 128:129, :], rbuf[n, 128:129, :]
             m = jnp.maximum(m1, m2)
             w1, w2 = jnp.exp2(m1 - m), jnp.exp2(m2 - m)
@@ -261,7 +260,6 @@
             total = bbuf[n, 129:130, :] * w1 + rbuf[n, 129:130, :] * w2
             bbuf[n, 128:129, :] = m
             bbuf[n, 129:130, :] = total
-            to_cross(g).start()
 
         def shared_place(m, c):
             return 4 + 2 * m + c
@@ -300,42 +298,43 @@
                 x_to_cross.wait_recv()
                 x_forward.start()
 
-        def before(i):
-            @pl.when(jnp.logical_and(i >= 4, i < GROUPS + 4))
-            def _():
-                combine_cross(i - 4)
-
-        def body(n, carry):
+        def combining(i):
+            to_partner(i - 2).wait_recv()
+
+            def beside(t):
+                if t == 1:
+                    combine_cross(i - 4)
+
+            return beside
+
+        def pair(n, combine):
             i = 2 + 2 * n
-            before(i)
-
-            @pl.when(n == 0)
-            def _():
-                wo_copy(0).start()
-                wo_copy(1).start()
-
-            attend(i, False)
-            before(i + 1)
+            attend(i, False, beside=combining(i) if combine else None)
+            if combine:
+                to_cross(i - 4).start()
+            beside = combining(i + 1) if combine else None
             for c in share(n, 1 - core):
                 c.wait_recv()
 
-            @pl.when(n < 2)
+            @pl.when(jnp.asarray(n) < 2)
             def _():
                 wq_copy(2 * (n + 2) + core).wait()
 
-            attend(i + 1, False, ahead=(shared_place(n + 1, core),))
+            attend(i + 1, False, ahead=(shared_place(n + 1, core),), beside=beside)
+            if combine:
+                to_cross(i - 3).start()
             for c in share(n + 1, core):
                 c.start()
 
-            @pl.when(n >= 2)
+            @pl.when(jnp.asarray(n) >= 2)
             def _():
                 wo_copy(2 * (n - 1) + core).start()
 
+        def body(n, carry):
+            pair(n, True)
             return carry
 
         def late_body(i, carry):
-            before(i)
-
             @pl.when(i == 2 * GROUPS - 3)
             def _():
                 for c in share(SHARED - 1, 1 - core):
@@ -353,7 +352,10 @@
         attend(1, False, ahead=(3, shared_place(0, core)))
         for c in share(0, core):
             c.start()
-        lax.fori_loop(0, 5, body, 0)
+        wo_copy(0).start()
+        wo_copy(1).start()
+        pair(0, False)
+        lax.fori_loop(1, 5, body, 0)
         lax.fori_loop(12, 15, late_body, 0)
 
         def slot_of(g):

time: 53.8 us -> 53.2 us (0.989)
  Pallas kernels: 53.1 us -> 52.5 us
    pallas_call x1, Pallas kernels: 52.3 us -> 51.7 us  [device_step(): pl.pallas_call(kernel, out_shape=(pltpu.VMEM((ROWS, HIDDEN), BF16), pltpu...]
where the time goes in v6:
time: 53.2 us; the launch traced here: 53.1 us
  Pallas kernels  52.5 us (99%)
  between operations  0.64 us (1%)
    pallas_call x1, Pallas kernels, device_step(): pl.pallas_call(kernel, out_shape=(pltpu.VMEM((ROWS, HIDDEN), BF16), pltpu...  51.7 us

profile of v6, /device:TPU:0, one launch (start us, length us, event | category | flops | bytes accessed | tf_op | source)
XLA Modules:
  0.0 53.1 jit_solution(1392613022610885269)
XLA Ops:
  0.6 51.7 %shard_map.139 = (bf16[64,2048]{1,0:T(8,128)(2,1)S(1)}, bf16[64,4,128]{2,1,0:T(4,128)(2,1)S(1)}, bf16[64,4,128]{2,1,0:T(4,128)(2,1)S(1)}) custom-call(bf16[64,2048]{1,0:T(8,128)(2,1)} %x_hbm.1, bf16[16384,128]{1,0:T(8,128)(2,1)} %bitcast.4, bf16[16384,128]{1,0:T(8,128)(2,1)} %bitcast.5, bf16[2048]{0:T(1024)(128)(2,1)} %ln_hbm.1, bf16[2048,4096]{1,0:T(8,128)(2,1)} %wq_hbm.1, ...), custom_call_target="tpu_custom_call" | custom-call | tf_op jit(solution)/shard_map/pallas_call | solution.py:455
  52.3 0.8 %shard_map.140 = (bf16[64,2048]{1,0:T(8,128)(2,1)}, bf16[64,4,128]{2,1,0:T(4,128)(2,1)}, bf16[64,4,128]{2,1,0:T(4,128)(2,1)}) custom-call(bf16[64,2048]{1,0:T(8,128)(2,1)S(1)} %get-tuple-element.6.refs_0_, bf16[64,4,128]{2,1,0:T(4,128)(2,1)S(1)} %get-tuple-element.7.refs_1_, bf16[64,4,128]{2,1,0:T(4,128)(2,1)S(1)} %get-tuple-element.8.refs_2_), custom_call_target="tpu_custom_call" | custom-call | tf_op jit(solution)/shard_map/pallas_call | solution.py:492
